TPU v7x, 32 devices: a whole 2x2x4 slice. The times are simulated.
32 devices in a mesh: mp: 4 (over z), latent: 8 (over y, x, core).
Axes of the slice: x: 2, y: 2, z: 4, core: 2. Of those that a mesh axis runs over, the one named last changes fastest.
Arguments:
- clean_stream: bfloat16 [128, 4608], P('latent', 'mp'), may hold values from -64 to 64
- patch_stream: bfloat16 [128, 4608], P('latent', 'mp'), may hold values from -64 to 64
- output_grad: bfloat16 [128, 4608], P('latent', 'mp'), may hold values from -1.5 to 1.5
- input_gain: float32 [4608], P('mp'), may hold values from 0.25 to 1.75
- gate_weight: bfloat16 [4608, 18432], P('mp', 'latent'), may hold values from -0.09375 to 0.09375
- up_weight: bfloat16 [4608, 18432], P('mp', 'latent'), may hold values from -0.09375 to 0.09375
- down_weight: bfloat16 [18432, 4608], P('latent', 'mp'), may hold values from -0.125 to 0.125
- output_gain: float32 [4608], P('mp'), may hold values from 0.25 to 1.75
- encoder_weight: bfloat16 [4608, 8192], P('mp', 'latent'), may hold values from -0.09375 to 0.09375
- encoder_bias: float32 [8192], P('latent'), may hold values from -1 to 0.3
- decoder_weight: bfloat16 [8192, 4608], P('latent', 'mp'), may hold values from -0.09375 to 0.09375
- decoder_bias: float32 [4608], P('mp'), may hold values from -3 to 3
- patch_positions: int32 [1, 8], replicated, may hold values from 0 to 127
Outputs:
- layer_output: bfloat16 [128, 4608], P('latent', 'mp')
- latent_effects: float32 [1, 8192], P(None, 'latent')
- position_effects: float32 [1, 8, 8192], P(None, None, 'latent')
All inputs are finite; a program needn't handle non-finite values.
Results may differ from a plain program's by a relative error of at most 0.017.
Values may be sent and summed in bfloat16 or wider, within the bound.
No kernel may reach another device: no remote copies, remote signals or barrier semaphores. Data moves between devices by JAX's collectives and lax.ppermute only.
A program may use at most 64 MiB of HBM per device.

v0:
```python
import jax
import jax.numpy as jnp
from jax import lax
from jax.sharding import PartitionSpec as P

D = 4608
SEQS = 1
SEQ = 128


epsilon = 1e-06
tanh_scale = 0.7978845608028654
cubic_term = 0.044715


def gelu_parts(gate_sum):
    inner = tanh_scale * (gate_sum + cubic_term * gate_sum * gate_sum * gate_sum)
    tangent = jnp.tanh(inner)
    gelu_value = 0.5 * gate_sum * (1.0 + tangent)
    gelu_slope = 0.5 * (1.0 + tangent) + 0.5 * gate_sum * (1.0 - tangent * tangent) * tanh_scale * (
        1.0 + 3.0 * cubic_term * gate_sum * gate_sum
    )
    return (gelu_value, gelu_slope)


def dot_transposed(left, right):
    return lax.dot_general(
        left, right, (((1,), (1,)), ((), ())), preferred_element_type=jnp.float32
    )


def per_device(
    clean_stream,
    patch_stream,
    output_grad,
    input_gain,
    gate_weight,
    up_weight,
    down_weight,
    output_gain,
    encoder_weight,
    encoder_bias,
    decoder_weight,
    decoder_bias,
    patch_positions,
):
    local_rows = clean_stream.shape[0]
    hidden_width = gate_weight.shape[1]
    latent_index = lax.axis_index("latent")
    clean_whole, patch_whole = (
        lax.all_gather(clean_stream, "latent", axis=0, tiled=True),
        lax.all_gather(patch_stream, "latent", axis=0, tiled=True),
    )
    clean_rows = clean_whole.astype(jnp.float32)
    centered_clean = (clean_rows - decoder_bias).astype(jnp.bfloat16)
    centered_patch = (patch_whole.astype(jnp.float32) - decoder_bias).astype(jnp.bfloat16)
    encode_clean = jnp.dot(centered_clean, encoder_weight, preferred_element_type=jnp.float32)
    encode_patch = jnp.dot(centered_patch, encoder_weight, preferred_element_type=jnp.float32)
    encode_clean, encode_patch = (
        lax.psum_scatter(
            encode_clean.astype(jnp.bfloat16), "mp", scatter_dimension=1, tiled=True
        ).astype(jnp.float32),
        lax.psum_scatter(
            encode_patch.astype(jnp.bfloat16), "mp", scatter_dimension=1, tiled=True
        ).astype(jnp.float32),
    )
    kept_width = encode_clean.shape[1]
    bias_part = lax.dynamic_slice_in_dim(
        encoder_bias, lax.axis_index("mp") * kept_width, kept_width, 0
    )
    feature_delta = jnp.maximum(encode_patch + bias_part, 0.0) - jnp.maximum(
        encode_clean + bias_part, 0.0
    )
    square_in = lax.psum(jnp.sum(clean_rows * clean_rows, axis=1), "mp")
    in_scale = lax.rsqrt(square_in / D + epsilon)[:, None]
    normed = (clean_rows * in_scale * input_gain).astype(jnp.bfloat16)
    normed_part = normed
    gate_up = lax.psum_scatter(
        jnp.concatenate(
            [
                jnp.dot(normed_part, gate_weight, preferred_element_type=jnp.float32),
                jnp.dot(normed_part, up_weight, preferred_element_type=jnp.float32),
            ],
            axis=1,
        ),
        "mp",
        scatter_dimension=0,
        tiled=True,
    )
    gate_sum = gate_up[:, :hidden_width]
    up_sum = gate_up[:, hidden_width:]
    gelu_value, gelu_slope = gelu_parts(gate_sum)
    hidden = (gelu_value * up_sum).astype(jnp.bfloat16)
    mlp_part = jnp.dot(
        lax.all_gather(hidden, "mp", axis=0, tiled=True),
        down_weight,
        preferred_element_type=jnp.float32,
    )
    mlp_out = lax.psum_scatter(mlp_part, "latent", scatter_dimension=0, tiled=True)
    grad_rows = output_grad.astype(jnp.float32)
    stream_rows = clean_stream.astype(jnp.float32)
    scale_rows = lax.dynamic_slice_in_dim(in_scale, latent_index * local_rows, local_rows, 0)
    weighted_out = output_gain * grad_rows
    square_out, cross_out = lax.psum(
        (jnp.sum(mlp_out * mlp_out, axis=1), jnp.sum(mlp_out * weighted_out, axis=1)), "mp"
    )
    out_scale = lax.rsqrt(square_out / D + epsilon)[:, None]
    block_rows = (stream_rows + mlp_out * out_scale * output_gain).astype(jnp.bfloat16)
    mlp_grad = (
        out_scale * weighted_out
        - mlp_out * out_scale * out_scale * out_scale * (cross_out / D)[:, None]
    ).astype(jnp.bfloat16)
    hidden_grad = dot_transposed(
        lax.all_gather(mlp_grad, "latent", axis=0, tiled=True), down_weight
    )
    hidden_grad_rows = lax.psum_scatter(hidden_grad, "mp", scatter_dimension=0, tiled=True)
    gate_grad = (hidden_grad_rows * up_sum * gelu_slope).astype(jnp.bfloat16)
    up_grad = (hidden_grad_rows * gelu_value).astype(jnp.bfloat16)
    joined_grad = jnp.concatenate([gate_grad, up_grad], axis=1)
    piece = lax.all_gather(joined_grad, "mp", axis=0, tiled=True)
    normed_part = dot_transposed(piece[:, :hidden_width], gate_weight) + dot_transposed(
        piece[:, hidden_width:], up_weight
    )
    normed_grad = lax.psum_scatter(normed_part, "latent", scatter_dimension=0, tiled=True)
    weighted_in = input_gain * normed_grad
    cross_in = lax.psum(jnp.sum(stream_rows * weighted_in, axis=1), "mp")
    site_rows = (
        grad_rows
        + scale_rows * weighted_in
        - stream_rows * scale_rows * scale_rows * scale_rows * (cross_in / D)[:, None]
    ).astype(jnp.bfloat16)
    site_grad = lax.all_gather(site_rows, "latent", axis=0, tiled=True)
    latent_grad = dot_transposed(site_grad, decoder_weight)
    offsets = jnp.arange(SEQS, dtype=jnp.int32)[:, None] * SEQ
    targets = patch_positions + offsets
    latent_grad = lax.psum_scatter(
        latent_grad.astype(jnp.bfloat16), "mp", scatter_dimension=1, tiled=True
    ).astype(jnp.float32)
    contribution = feature_delta * latent_grad
    totals = jnp.sum(contribution.reshape(SEQS, SEQ, kept_width), axis=1)
    picked = contribution[targets]
    latent_effects, position_effects = (
        lax.all_gather(totals, "mp", axis=1, tiled=True),
        lax.all_gather(picked, "mp", axis=2, tiled=True),
    )
    return (block_rows, latent_effects, position_effects)


def solution(mesh):
    in_specs = (
        P("latent", "mp"),
        P("latent", "mp"),
        P("latent", "mp"),
        P("mp"),
        P("mp", "latent"),
        P("mp", "latent"),
        P("latent", "mp"),
        P("mp"),
        P("mp", "latent"),
        P("latent"),
        P("latent", "mp"),
        P("mp"),
        P(),
    )
    out_specs = (P("latent", "mp"), P(None, "latent"), P(None, None, "latent"))
    return jax.shard_map(
        per_device, mesh=mesh, in_specs=in_specs, out_specs=out_specs, check_vma=False
    )
```

profile of v0, /device:TPU:0, one launch (start us, length us, event | category | flops | bytes accessed | tf_op | source)
XLA Modules:
  0.0 361.6 jit_solution(685665116333672103)
XLA Ops:
  7.2 11.3 %all_gather.24 = bf16[128,1152]{1,0:T(8,128)(2,1)S(1)} all-gather(bf16[16,1152]{1,0:T(8,128)(2,1)} %param.13), channel_id=1, replica_groups=mesh['mp'=4,'latent'=8] {'latent'}, dimensions={0}, use_global_device_ids=true | all-gather | bytes 331776 | tf_op jit(solution)/shard_map/all_gather | solution.py:51
  18.6 12.0 %psum.28 = f32[128]{0:T(128)S(1)} all-reduce(f32[128]{0:T(128)S(1)} %fusion), channel_id=1, replica_groups=mesh['mp'=4,'latent'=8] {'mp'}, use_global_device_ids=true, to_apply=%region_1.0 | all-reduce | flops 128 | bytes 1024 | tf_op jit(solution)/shard_map/psum | solution.py:74
  30.6 3.7 %fusion.19 = f32[128,2304]{1,0:T(8,128)S(1)} fusion(bf16[1152,2304]{1,0:T(8,128)(2,1)} %param.18, bf16[128,1152]{1,0:T(8,128)(2,1)S(1)} %all_gather.24, f32[1152]{0:T(1024)} %param.16, f32[128]{0:T(128)S(1)} %add_rsqrt_fusion.1), kind=kOutput, calls=%fused_computation.40 | convolution fusion | flops 680067072 | bytes 6788096 | tf_op jit(solution)/shard_map/dot_general | solution.py:82
  35.7 1.7 pad_maximum_fusion
  37.5 45.0 %reduce-scatter.8.cloned.1.call-done = f32[32,4608]{1,0:T(8,128)} async-done(((f32[128,4608]{1,0:T(8,128)}), f32[32,4608]{1,0:T(8,128)}) %reduce-scatter.8.cloned.1.call-update) | async-done | bytes 589840 | tf_op jit(solution)/shard_map/reduce_scatter | solution.py:78
  83.6 15.4 %all_gather.25 = bf16[128,2304]{1,0:T(8,128)(2,1)S(1)} all-gather(bf16[32,2304]{1,0:T(8,128)(2,1)S(1)} %multiply_convert_fusion.1), channel_id=1, replica_groups=mesh['mp'=4,'latent'=8] {'mp'}, dimensions={0}, use_global_device_ids=true | all-gather | bytes 737280 | tf_op jit(solution)/shard_map/all_gather | solution.py:95
  99.0 4.3 %fusion.35 = f32[128,1152]{1,0:T(8,128)} fusion(bf16[128,2304]{1,0:T(8,128)(2,1)S(1)} %all_gather.25, bf16[2304,1152]{1,0:T(8,128)(2,1)} %param.19), kind=kOutput, calls=%fused_computation.61 | convolution fusion | flops 679477248 | bytes 6488064 | tf_op jit(solution)/shard_map/dot_general | solution.py:94
  103.4 34.5 %reduce-scatter.10.cloned.1.call-done = f32[16,1152]{1,0:T(8,128)} async-done(((f32[128,1152]{1,0:T(8,128)}), f32[16,1152]{1,0:T(8,128)}) %reduce-scatter.10.cloned.1.call-update) | async-done | bytes 73744 | tf_op jit(solution)/shard_map/reduce_scatter | solution.py:99
  138.9 11.7 %all-reduce = (f32[16]{0:T(128)S(1)}, f32[16]{0:T(128)S(1)}) all-reduce(f32[16]{0:T(128)S(1)} %get-tuple-element.4, f32[16]{0:T(128)S(1)} %get-tuple-element.3), channel_id=1, replica_groups=mesh['mp'=4,'latent'=8] {'mp'}, use_global_device_ids=true, to_apply=%region_5.0 | all-reduce | flops 32 | bytes 256 | tf_op jit(solution)/shard_map/psum | solution.py:104
  152.1 9.4 %all_gather.27 = bf16[128,1152]{1,0:T(8,128)(2,1)S(1)} all-gather(bf16[16,1152]{1,0:T(8,128)(2,1)S(1)} %get-tuple-element.11), channel_id=1, replica_groups=mesh['mp'=4,'latent'=8] {'latent'}, dimensions={0}, use_global_device_ids=true | all-gather | bytes 331776 | tf_op jit(solution)/shard_map/all_gather | solution.py:114
  161.5 5.1 %fusion.36 = f32[128,2304]{1,0:T(8,128)} fusion(bf16[128,1152]{1,0:T(8,128)(2,1)S(1)} %all_gather.27, bf16[2304,1152]{1,0:T(8,128)(2,1)} %param.19), kind=kOutput, calls=%fused_computation.62 | convolution fusion | flops 679477248 | bytes 6782976 | tf_op jit(solution)/shard_map/dot_general | solution.py:27
  166.7 26.7 %reduce-scatter.16.cloned.1.call-done = f32[32,2304]{1,0:T(8,128)} async-done(((f32[128,2304]{1,0:T(8,128)}), f32[32,2304]{1,0:T(8,128)}) %reduce-scatter.16.cloned.1.call-update) | async-done | bytes 294928 | tf_op jit(solution)/shard_map/reduce_scatter | solution.py:116
  195.4 29.0 %all-gather.5.cloned.1.call-done = bf16[128,4608]{1,0:T(8,128)(2,1)} async-done(((bf16[32,4608]{1,0:T(8,128)(2,1)}), bf16[128,4608]{1,0:T(8,128)(2,1)}) %all-gather.5.cloned.1.call-update) | async-done | bytes 1179664 | tf_op jit(solution)/shard_map/all_gather | solution.py:120
  224.4 4.5 %fusion.5 = f32[128,1152]{1,0:T(8,128)S(1)} fusion(bf16[1152,2304]{1,0:T(8,128)(2,1)} %param.17, bf16[128,4608]{1,0:T(8,128)(2,1)} %all-gather.5.cloned.1.call-done), kind=kOutput, calls=%fused_computation.14 | convolution fusion | flops 679477248 | bytes 6488064 | tf_op jit(solution)/shard_map/dot_general | solution.py:27
  228.9 5.1 %convolution_add_fusion = f32[128,1152]{1,0:T(8,128)} fusion(f32[128,1152]{1,0:T(8,128)S(1)} %fusion.5, bf16[1152,2304]{1,0:T(8,128)(2,1)} %param.18, bf16[128,4608]{1,0:T(8,128)(2,1)S(1)} %copy-done.3), kind=kOutput, calls=%fused_computation.1 | convolution fusion | flops 679624704 | bytes 7077888 | tf_op jit(solution)/shard_map/dot_general | solution.py:27
  235.4 9.4 %all_gather.26 = bf16[128,1152]{1,0:T(8,128)(2,1)S(1)} all-gather(bf16[16,1152]{1,0:T(8,128)(2,1)S(1)} %copy-done.7), channel_id=1, replica_groups=mesh['mp'=4,'latent'=8] {'latent'}, dimensions={0}, use_global_device_ids=true | all-gather | bytes 331776 | tf_op jit(solution)/shard_map/all_gather | solution.py:52
  246.2 21.6 %reduce-scatter.18.cloned.1.call-done = f32[16,1152]{1,0:T(8,128)} async-done(((f32[128,1152]{1,0:T(8,128)}), f32[16,1152]{1,0:T(8,128)}) %reduce-scatter.18.cloned.1.call-update) | async-done | bytes 73744 | tf_op jit(solution)/shard_map/reduce_scatter | solution.py:124
  268.7 11.7 %psum.31 = f32[16]{0:T(128)S(1)} all-reduce(f32[16]{0:T(128)S(1)} %fusion.32), channel_id=1, replica_groups=mesh['mp'=4,'latent'=8] {'mp'}, use_global_device_ids=true, to_apply=%region_13.0 | all-reduce | flops 16 | bytes 128 | tf_op jit(solution)/shard_map/psum | solution.py:126
  281.4 9.4 %all_gather.29 = bf16[128,1152]{1,0:T(8,128)(2,1)S(1)} all-gather(bf16[16,1152]{1,0:T(8,128)(2,1)S(1)} %fusion.27), channel_id=1, replica_groups=mesh['mp'=4,'latent'=8] {'latent'}, dimensions={0}, use_global_device_ids=true | all-gather | bytes 331776 | tf_op jit(solution)/shard_map/all_gather | solution.py:132
  290.8 3.2 convolution_convert_fusion
  294.9 15.5 %reduce-scatter.12.cloned.1.call-done = bf16[128,256]{1,0:T(8,128)(2,1)} async-done(((bf16[128,1024]{1,0:T(8,128)(2,1)}), bf16[128,256]{1,0:T(8,128)(2,1)}) %reduce-scatter.12.cloned.1.call-update) | async-done | bytes 65552 | tf_op jit(solution)/shard_map/reduce_scatter | solution.py:63
  310.4 20.5 %reduce-scatter.20.cloned.1.call-done = bf16[128,256]{1,0:T(8,128)(2,1)} async-done(((bf16[128,1024]{1,0:T(8,128)(2,1)}), bf16[128,256]{1,0:T(8,128)(2,1)}) %reduce-scatter.20.cloned.1.call-update) | async-done | bytes 65552 | tf_op jit(solution)/shard_map/reduce_scatter | solution.py:136
  331.9 8.0 %all-gather.2 = f32[4,1,256]{2,1,0:T(1,128)S(1)} all-gather(f32[1,1,256]{2,1,0:T(1,128)S(1)} %bitcast.19), channel_id=2, replica_groups=mesh['mp'=4,'latent'=8] {'mp'}, dimensions={0}, use_global_device_ids=true | all-gather | bytes 5120 | tf_op jit(solution)/shard_map/all_gather | solution.py:143
  340.4 13.1 %all-gather.1 = f32[8,1024]{1,0:T(8,128)S(1)} all-gather(f32[8,256]{1,0:T(8,128)S(1)} %gather_fusion), channel_id=3, replica_groups=mesh['mp'=4,'latent'=8] {'mp'}, dimensions={1}, use_global_device_ids=true | all-gather | bytes 40960 | tf_op jit(solution)/shard_map/all_gather | solution.py:144
  (61 shorter events, 15.8 us)
Async XLA Ops:
  7.2 226.9 %copy-start = (bf16[1152,1024]{1,0:T(8,128)(2,1)S(1)}, bf16[1152,1024]{1,0:T(8,128)(2,1)}, u32[]{:S(2)}) copy-start(bf16[1152,1024]{1,0:T(8,128)(2,1)} %param.21) | copy-start | bytes 7077892
  7.2 75.3 %reduce-scatter.8.cloned.1.call-start = ((), (), s32[]{:S(2)}) async-start(), calls=%async_computation.7 | async-start | bytes 2949120 | tf_op jit(solution)/shard_map/reduce_scatter | solution.py:78
  30.6 4.1 %copy-start.1 = (bf16[1152,2304]{1,0:T(8,128)(2,1)S(1)}, bf16[1152,2304]{1,0:T(8,128)(2,1)}, u32[]{:S(2)}) copy-start(bf16[1152,2304]{1,0:T(8,128)(2,1)} %param.17) | copy-start | bytes 15925252
  30.6 4.1 %copy-start.6 = (f32[1152]{0:T(1024)S(1)}, f32[1152]{0:T(1024)}, u32[]{:S(2)}) copy-start(f32[1152]{0:T(1024)} %param.16) | copy-start | bytes 13828
  37.4 100.4 %reduce-scatter.10.cloned.1.call-start = ((), (), s32[]{:S(2)}) async-start(), calls=%async_computation.8 | async-start | bytes 663552 | tf_op jit(solution)/shard_map/reduce_scatter | solution.py:99
  99.0 38.8 %copy-start.5 = (bf16[16,1152]{1,0:T(8,128)(2,1)S(1)}, bf16[16,1152]{1,0:T(8,128)(2,1)}, u32[]{:S(2)}) copy-start(bf16[16,1152]{1,0:T(8,128)(2,1)} %param.15) | copy-start | bytes 110596
  99.0 38.8 %copy-start.9 = (f32[1152]{0:T(1024)S(1)}, f32[1152]{0:T(1024)}, u32[]{:S(2)}) copy-start(f32[1152]{0:T(1024)} %param.20) | copy-start | bytes 13828
  99.0 51.5 %copy-start.4 = (bf16[16,1152]{1,0:T(8,128)(2,1)S(1)}, bf16[16,1152]{1,0:T(8,128)(2,1)}, u32[]{:S(2)}) copy-start(bf16[16,1152]{1,0:T(8,128)(2,1)} %param.13) | copy-start | bytes 110596
  103.3 90.1 %reduce-scatter.16.cloned.1.call-start = ((), (), s32[]{:S(2)}) async-start(), calls=%async_computation.11 | async-start | bytes 1474560 | tf_op jit(solution)/shard_map/reduce_scatter | solution.py:116
  161.5 31.9 %copy-start.2 = (f32[32,4608]{1,0:T(8,128)S(1)}, f32[32,4608]{1,0:T(8,128)}, u32[]{:S(2)}) copy-start(f32[32,4608]{1,0:T(8,128)} %reduce-scatter.8.cloned.1.call-done) | copy-start | bytes 1769476
  166.7 57.7 %all-gather.5.cloned.1.call-start = ((), (), s32[]{:S(2)}) async-start(), calls=%async_computation.12 | async-start | bytes 1474560 | tf_op jit(solution)/shard_map/all_gather | solution.py:120
  195.3 72.4 %reduce-scatter.18.cloned.1.call-start = ((), (), s32[]{:S(2)}) async-start(), calls=%async_computation.13 | async-start | bytes 663552 | tf_op jit(solution)/shard_map/reduce_scatter | solution.py:124
  224.4 4.5 %copy-start.3 = (bf16[128,4608]{1,0:T(8,128)(2,1)S(1)}, bf16[128,4608]{1,0:T(8,128)(2,1)}, u32[]{:S(2)}) copy-start(bf16[128,4608]{1,0:T(8,128)(2,1)} %all-gather.5.cloned.1.call-done) | copy-start | bytes 3538948
  228.9 5.2 %copy-start.8 = (f32[1152]{0:T(1024)S(1)}, f32[1152]{0:T(1024)}, u32[]{:S(2)}) copy-start(f32[1152]{0:T(1024)} %param.24) | copy-start | bytes 13828
  234.0 1.4 copy-start.7
  234.1 60.8 %reduce-scatter.14.cloned.1.call-start = ((), (), s32[]{:S(2)}) async-start(), calls=%async_computation.10 | async-start | bytes 327680 | tf_op jit(solution)/shard_map/reduce_scatter | solution.py:60
  235.4 75.0 %reduce-scatter.12.cloned.1.call-start = ((), (), s32[]{:S(2)}) async-start(), calls=%async_computation.9 | async-start | bytes 327680 | tf_op jit(solution)/shard_map/reduce_scatter | solution.py:63
  246.0 48.8 %copy-start.10 = (s32[1,8]{1,0:T(1,128)S(1)}, s32[1,8]{1,0:T(1,128)}, u32[]{:S(2)}) copy-start(s32[1,8]{1,0:T(1,128)} %param.25) | copy-start | bytes 100
  246.1 84.8 %reduce-scatter.20.cloned.1.call-start = ((), (), s32[]{:S(2)}) async-start(), calls=%async_computation.14 | async-start | bytes 327680 | tf_op jit(solution)/shard_map/reduce_scatter | solution.py:136
Sparse Core Ops, SparseCore 0:
  37.5 44.8 reduce-scatter.7
  103.4 34.3 reduce-scatter.9
  166.8 26.5 reduce-scatter.15
  195.5 28.8 all-gather.4
  234.2 33.5 reduce-scatter.17
  269.9 19.9 reduce-scatter.13
  292.1 18.2 reduce-scatter.11
  312.6 18.2 reduce-scatter.19
where the time goes:
time: 362 us
  waiting for transfers between devices  193 us (53%)
  blocking collectives  111 us (31%)
  matrix products  29.4 us (8%)
  between operations  14.3 us (4%)
  other arithmetic  10.5 us (3%)
    reduce_scatter x1, waiting for transfers between devices, per_device(): lax.psum_scatter(jnp.concatenate([jnp.dot(normed_part, gate_weight, prefe...  45 us
    reduce_scatter x1, waiting for transfers between devices, per_device(): lax.psum_scatter(mlp_part, 'latent', scatter_dimension=0, tiled=True)  34.5 us
    all_gather x1, waiting for transfers between devices, per_device(): piece = lax.all_gather(joined_grad, 'mp', axis=0, tiled=True)  29 us
    reduce_scatter x1, waiting for transfers between devices, per_device(): lax.psum_scatter(hidden_grad, 'mp', scatter_dimension=0, tiled=True)  26.7 us
    reduce_scatter x1, waiting for transfers between devices, per_device(): lax.psum_scatter(normed_part, 'latent', scatter_dimension=0, tiled=True)  21.6 us
    reduce_scatter x1, waiting for transfers between devices, per_device(): lax.psum_scatter(latent_grad.astype(jnp.bfloat16), 'mp', scatter_dimensio...  20.5 us
    dot_general x4, matrix products, dot_transposed(): lax.dot_general(left, right, (((1,), (1,)), ((), ())), preferred_element_...  18 us
    reduce_scatter x1, waiting for transfers between devices, per_device(): lax.psum_scatter(encode_patch.astype(jnp.bfloat16), 'mp', scatter_dimensi...  15.5 us
  transfers between devices with their start and end apart: 8, of which 7 were waited for; matrix products, arithmetic and copies ran while one was open for 2% of the time, Pallas kernels for 0%

commit v1 on v0

v1 whole, which is shorter than its diff:
```python
import jax
import jax.numpy as jnp
from jax import lax
from jax.sharding import PartitionSpec as P


epsilon = 1e-06
tanh_scale = 0.7978845608028654
cubic_term = 0.044715
LANES = 128
f32 = jnp.float32
bf16 = jnp.bfloat16


def gelu_parts(gate_sum):
    inner = tanh_scale * (gate_sum + cubic_term * gate_sum * gate_sum * gate_sum)
    tangent = jnp.tanh(inner)
    gelu_value = 0.5 * gate_sum * (1.0 + tangent)
    gelu_slope = 0.5 * (1.0 + tangent) + 0.5 * gate_sum * (1.0 - tangent * tangent) * tanh_scale * (
        1.0 + 3.0 * cubic_term * gate_sum * gate_sum
    )
    return (gelu_value, gelu_slope)


def dot(left, right):
    return jnp.dot(left, right, preferred_element_type=f32)


def dot_transposed(left, right):
    return lax.dot_general(left, right, (((1,), (1,)), ((), ())), preferred_element_type=f32)


def swap(value, axis, distance):
    count = lax.axis_size(axis)
    return lax.ppermute(value, axis, [(i, i ^ distance) for i in range(count)])


def split_columns(columns):
    rows = columns[0].shape[0]
    lane = lax.broadcasted_iota(jnp.int32, (rows, LANES), 1)
    block = jnp.zeros((rows, LANES), f32)
    for index, column in enumerate(columns):
        high = lax.reduce_precision(column, 8, 7)
        rest = column - high
        middle = lax.reduce_precision(rest, 8, 7)
        for part, piece in enumerate((high, middle, rest - middle)):
            block = jnp.where(lane == 3 * index + part, piece, block)
    return block.astype(bf16)


def join_columns(block, count):
    lane = lax.broadcasted_iota(jnp.int32, block.shape, 1)
    wide = block.astype(f32)
    return [
        jnp.sum(jnp.where(lane // 3 == index, wide, 0.0), axis=1, keepdims=True)
        for index in range(count)
    ]


def scatter_mp(partial):
    count = lax.axis_size("mp")
    rows = partial.shape[0] // count
    got = []
    for m in range(1, count):
        got.append(swap(partial[m * rows : (m + 1) * rows], "mp", m))
    return got


def gather_mp(block):
    blocks = [block]
    for m in range(1, lax.axis_size("mp")):
        blocks.append(swap(block, "mp", m))
    return jnp.concatenate(blocks, axis=0)


def reduce_latent(partial, extra):
    count = lax.axis_size("latent")
    side = lax.axis_index("latent") % 2 == 0
    half = partial.shape[0] // 2
    width = partial.shape[1]

    def pack(main, column):
        return main if column is None else jnp.concatenate([main, split_columns([column])], axis=1)

    def add(main, column, got):
        total = (main.astype(f32) + got[:, :width].astype(f32)).astype(bf16)
        return total, None if column is None else column + join_columns(got[:, width:], 1)[0]

    def pick(value, first):
        return jnp.where(first, value[:half], value[half:])

    main, column = pick(partial, side), None if extra is None else pick(extra, side)
    sent = pack(pick(partial, ~side), None if extra is None else pick(extra, ~side))
    got = swap(sent, "latent", 1)
    main, column = add(main, column, got)
    distances = [1 << bit for bit in range(1, count.bit_length() - 1)]
    quarter = half // 2
    done = []
    for lower, order in ((0, distances), (quarter, distances[::-1])):
        done.append(
            [main[lower : lower + quarter], None if column is None else column[lower : lower + quarter], order]
        )
    for step in range(len(distances)):
        got = [swap(pack(m, c), "latent", order[step]) for m, c, order in done]
        done = [[*add(m, c, g), order] for (m, c, order), g in zip(done, got)]
    main = jnp.concatenate([d[0] for d in done], axis=0)
    column = None if extra is None else jnp.concatenate([d[1] for d in done], axis=0)
    other = swap(pack(main, column), "latent", 1)
    low = jnp.where(side, main, other[:, :width])
    high = jnp.where(side, other[:, :width], main)
    total = jnp.concatenate([low, high], axis=0)
    if extra is None:
        return total, None
    far = join_columns(other[:, width:], 1)[0]
    return total, jnp.concatenate([jnp.where(side, column, far), jnp.where(side, far, column)], axis=0)


def program(
    clean_stream,
    patch_stream,
    output_grad,
    input_gain,
    gate_weight,
    up_weight,
    down_weight,
    output_gain,
    encoder_weight,
    encoder_bias,
    decoder_weight,
    decoder_bias,
    patch_positions,
):
    mp_count = lax.axis_size("mp")
    mp_index = lax.axis_index("mp")
    latent_index = lax.axis_index("latent")
    local_rows = clean_stream.shape[0]
    model_width = clean_stream.shape[1] * mp_count
    hidden_width = gate_weight.shape[1]
    tokens = local_rows * lax.axis_size("latent")
    rows = tokens // mp_count

    def by_distance(whole):
        return jnp.concatenate(
            [lax.dynamic_slice_in_dim(whole, (mp_index ^ m) * rows, rows, 0) for m in range(mp_count)], axis=0
        )

    clean = by_distance(lax.all_gather(clean_stream, "latent", axis=0, tiled=True))
    clean_rows = clean.astype(f32)
    square_part = jnp.sum(clean_rows * clean_rows, axis=1, keepdims=True)
    scaled = (clean_rows * input_gain).astype(bf16)
    gate_part = dot(scaled, gate_weight)
    up_part = dot(scaled, up_weight)
    sent = jnp.concatenate(
        [gate_part.astype(bf16), up_part.astype(bf16), split_columns([square_part])], axis=1
    )
    got = scatter_mp(sent)

    other_rows = jnp.concatenate([output_grad, patch_stream], axis=0)
    other_rows, _ = lax.optimization_barrier((other_rows, sent))
    others = lax.all_gather(other_rows, "latent", axis=0)
    got, others = lax.optimization_barrier((got, others))
    grad = by_distance(others[:, :local_rows].reshape(tokens, -1))
    patch = by_distance(others[:, local_rows:].reshape(tokens, -1))

    def total(part, pieces, begin):
        end = begin + part.shape[1]
        value = part[:rows]
        for piece in pieces:
            value = value + piece[:, begin:end].astype(f32)
        return value

    square_in = square_part[:rows]
    for piece in got:
        square_in = square_in + join_columns(piece[:, 2 * hidden_width :], 1)[0]
    in_scale = lax.rsqrt(square_in / model_width + epsilon)
    gate_sum = total(gate_part, got, 0) * in_scale
    up_sum = total(up_part, got, hidden_width) * in_scale
    gelu_value, gelu_slope = gelu_parts(gate_sum)
    gate_factor = up_sum * gelu_slope
    hidden = (gelu_value * up_sum).astype(bf16)
    radial = gate_factor * gate_sum + gelu_value * up_sum
    hidden_all = gather_mp(hidden)

    grad_rows = grad.astype(f32)
    weighted_out = output_gain * grad_rows
    linear_part = dot_transposed(weighted_out.astype(bf16), down_weight)
    linear_sent = linear_part.astype(bf16)
    encode_clean = dot((clean_rows - decoder_bias).astype(bf16), encoder_weight)
    encode_patch = dot((patch.astype(f32) - decoder_bias).astype(bf16), encoder_weight)
    clean_sent, patch_sent = encode_clean.astype(bf16), encode_patch.astype(bf16)
    linear_sent, clean_sent, hidden_all = lax.optimization_barrier((linear_sent, clean_sent, hidden_all))
    linear_got = scatter_mp(linear_sent)
    clean_got = scatter_mp(clean_sent)

    mlp_part = dot(hidden_all, down_weight).astype(bf16)
    mlp_out, _ = reduce_latent(mlp_part, None)
    mlp_rows = mlp_out.astype(f32)
    square_out = jnp.sum(mlp_rows * mlp_rows, axis=1, keepdims=True)
    cross_out = jnp.sum(mlp_rows * weighted_out, axis=1, keepdims=True)
    back_part = dot_transposed(mlp_out, down_weight)
    back_got = scatter_mp(jnp.concatenate([back_part.astype(bf16), split_columns([square_out, cross_out])], axis=1))
    square_own, cross_own = square_out[:rows], cross_out[:rows]
    for piece in back_got:
        square_piece, cross_piece = join_columns(piece[:, hidden_width:], 2)
        square_own, cross_own = square_own + square_piece, cross_own + cross_piece
    out_scale = lax.rsqrt(square_own / model_width + epsilon)
    hidden_grad = out_scale * total(linear_part, linear_got, 0) - (
        out_scale * out_scale * out_scale * (cross_own / model_width)
    ) * total(back_part, back_got, 0)
    gate_grad = (hidden_grad * gate_factor).astype(bf16)
    up_grad = (hidden_grad * gelu_value).astype(bf16)
    cross_in = jnp.sum(hidden_grad * radial, axis=1, keepdims=True)
    grads = gather_mp(jnp.concatenate([gate_grad, up_grad, split_columns([cross_in, in_scale, out_scale])], axis=1))
    cross_in, in_scale, out_scale = join_columns(grads[:, 2 * hidden_width :], 3)

    own_row = latent_index * local_rows
    own_row = (mp_index ^ (own_row // rows)) * rows + own_row % rows
    own = lambda value: lax.dynamic_slice_in_dim(value, own_row, local_rows, 0)
    block_rows = (
        clean_stream.astype(f32) + own(mlp_out).astype(f32) * own(out_scale) * output_gain
    ).astype(bf16)

    patch_sent, grads = lax.optimization_barrier((patch_sent, grads))
    patch_got = scatter_mp(patch_sent)
    latents = encoder_weight.shape[1]
    feature_delta = jnp.maximum(total(encode_patch, patch_got, 0) + encoder_bias, 0.0) - jnp.maximum(
        total(encode_clean, clean_got, 0) + encoder_bias, 0.0
    )
    feature_delta = gather_mp(feature_delta.astype(bf16)).astype(f32)

    normed_part = dot_transposed(grads[:, :hidden_width], gate_weight) + dot_transposed(
        grads[:, hidden_width : 2 * hidden_width], up_weight
    )
    normed_grad, cross_in = reduce_latent(normed_part.astype(bf16), cross_in)
    site_grad = (
        grad_rows
        + in_scale * (input_gain * normed_grad.astype(f32))
        - clean_rows * (in_scale * in_scale * (cross_in / model_width))
    ).astype(bf16)
    contribution = feature_delta * dot_transposed(site_grad, decoder_weight)

    sequences, picks = patch_positions.shape
    length = tokens // sequences
    targets = patch_positions + jnp.arange(sequences, dtype=jnp.int32)[:, None] * length
    targets = (mp_index ^ (targets // rows)) * rows + targets % rows
    token = (mp_index ^ (jnp.arange(tokens, dtype=jnp.int32) // rows)) * rows + jnp.arange(
        tokens, dtype=jnp.int32
    ) % rows
    inside = [(token // length == s)[:, None] for s in range(sequences)]
    chosen = [jnp.where(m, 1.0, 0.0).reshape(1, -1) for m in inside]
    chosen.append((targets.reshape(-1, 1) == jnp.arange(tokens, dtype=jnp.int32)[None]).astype(f32))
    effects = jnp.dot(jnp.concatenate(chosen, axis=0), contribution, precision=lax.Precision.HIGHEST)
    distance = 1
    while distance < mp_count:
        effects = effects + swap(effects, "mp", distance)
        distance *= 2
    return (block_rows, effects[:sequences], effects[sequences:].reshape(sequences, picks, latents))


def solution(mesh):
    in_specs = (
        P("latent", "mp"),
        P("latent", "mp"),
        P("latent", "mp"),
        P("mp"),
        P("mp", "latent"),
        P("mp", "latent"),
        P("latent", "mp"),
        P("mp"),
        P("mp", "latent"),
        P("latent"),
        P("latent", "mp"),
        P("mp"),
        P(),
    )
    out_specs = (P("latent", "mp"), P(None, "latent"), P(None, None, "latent"))
    return jax.shard_map(program, mesh=mesh, in_specs=in_specs, out_specs=out_specs, check_vma=False)
```

time: 362 us -> 186 us (0.51)
  waiting for transfers between devices: 193 us -> 76.5 us
  blocking collectives: 111 us -> 21.2 us
  starting transfers between devices: 0.33 us -> 53.9 us
  between operations: 14.3 us -> 1.49 us
  matrix products: 29.4 us -> 19.3 us
    reduce_scatter x7 -> x0, waiting for transfers between devices: 164 us -> none  [the longest x1 45 us: per_device(): lax.psum_scatter(jnp.concatenate([jnp.dot(normed_part, gate_weight, prefe...]
    ppermute x0 -> x38, waiting for transfers between devices: none -> 76.5 us  [swap(): return lax.ppermute(value, axis, [(i, i ^ distance) for i in range(count)])]
    all_gather x7 -> x2, blocking collectives: 76 us -> 21.2 us  [the longest x1 11.3 us: program(): lax.all_gather(clean_stream, 'latent', axis=0, tiled=True)]
    ppermute x0 -> x38, starting transfers between devices: none -> 53.9 us  [swap(): return lax.ppermute(value, axis, [(i, i ^ distance) for i in range(count)])]
    psum x3 -> x0, blocking collectives: 35.3 us -> none  [the longest x1 12 us: per_device(): square_in = lax.psum(jnp.sum(clean_rows * clean_rows, axis=1), 'mp')]
    all_gather x1 -> x0, waiting for transfers between devices: 29 us -> none  [per_device(): piece = lax.all_gather(joined_grad, 'mp', axis=0, tiled=True)]
    dot_general x4 -> x5, matrix products: 18 us -> 10.3 us  [dot_transposed(): lax.dot_general(left, right, (((1,), (1,)), ((), ())), preferred_element_...]
    dot_general x5 -> x6, matrix products: 11.4 us -> 9.03 us  [the longest x5 8.63 us: dot(): return jnp.dot(left, right, preferred_element_type=f32)]
  transfers between devices with their start and end apart: 8 -> 38, of which waited for: 7 -> 23; matrix products, arithmetic and copies ran while one was open for 2% -> 6% of each run, Pallas kernels for 0% -> 0%
where the time goes in v1:
time: 186 us; the launch traced here: 185 us
  waiting for transfers between devices  76.5 us (41%)
  starting transfers between devices  53.9 us (29%)
  blocking collectives  21.2 us (11%)
  matrix products  19.3 us (10%)
  other arithmetic  10.2 us (5%)
  local copies, waits for them, and re-layouts  2.63 us (1%)
    ppermute x38, waiting for transfers between devices, swap(): return lax.ppermute(value, axis, [(i, i ^ distance) for i in range(count)])  76.5 us
    ppermute x38, starting transfers between devices, swap(): return lax.ppermute(value, axis, [(i, i ^ distance) for i in range(count)])  53.9 us
    all_gather x1, blocking collectives, program(): lax.all_gather(clean_stream, 'latent', axis=0, tiled=True)  11.3 us
    dot_general x5, matrix products, dot_transposed(): lax.dot_general(left, right, (((1,), (1,)), ((), ())), preferred_element_...  10.3 us
    all_gather x1, blocking collectives, program(): others = lax.all_gather(other_rows, 'latent', axis=0)  9.92 us
    dot_general x5, matrix products, dot(): return jnp.dot(left, right, preferred_element_type=f32)  8.63 us
  transfers between devices with their start and end apart: 38, of which 23 were waited for; matrix products, arithmetic and copies ran while one was open for 6% of the time, Pallas kernels for 0%

profile of v1, /device:TPU:0, one launch (start us, length us, event | category | flops | bytes accessed | tf_op | source)
XLA Modules:
  0.0 185.3 jit_solution(2371385495379136915)
XLA Ops:
  1.2 11.3 %all_gather.9 = bf16[128,1152]{1,0:T(8,128)(2,1)S(1)} all-gather(bf16[16,1152]{1,0:T(8,128)(2,1)} %param.13), channel_id=1, replica_groups=mesh['mp'=4,'latent'=8] {'latent'}, dimensions={0}, use_global_device_ids=true | all-gather | bytes 331776 | tf_op jit(solution)/shard_map/all_gather | solution.py:147
  12.7 4.7 %fusion.134 = (bf16[128,2304]{1,0:T(8,128)(2,1)S(1)}, f32[128,2304]{1,0:T(8,128)}) fusion(bf16[1152,2304]{1,0:T(8,128)(2,1)} %param.18, f32[1152]{0:T(1024)} %param.16, bf16[32,1152]{1,0:T(8,128)(2,1)S(1)} %get-tuple-element.88, bf16[32,1152]{1,0:T(8,128)(2,1)S(1)} %get-tuple-element.89, bf16[32,1152]{1,0:T(8,128)(2,1)S(1)} %get-tuple-element.90, ...), kind=kOutput, calls=%fused_computation.293 | convolution fusion | flops 681246720 | bytes 7377408 | tf_op jit(solution)/shard_map/dot_general | solution.py:26
  22.1 2.6 %collective-permute-start.1 = (bf16[32,4736]{1,0:T(8,128)(2,1)}, bf16[32,4736]{1,0:T(8,128)(2,1)}, u32[]{:S(2)}, u32[]{:S(2)}) collective-permute-start(bf16[32,4736]{1,0:T(8,128)(2,1)} %get-tuple-element.63), channel_id=1, source_target_pairs={{0,16},{8,24},{16,0},{24,8},{1,17},{9,25},{17,1},{25,9},{2,18},{10... | collective-permute-start | bytes 909320 | tf_op jit(solution)/shard_map/ppermute | solution.py:35
  26.1 9.9 %all-gather = bf16[256,1152]{1,0:T(8,128)(2,1)S(1)} all-gather(bf16[32,1152]{1,0:T(8,128)(2,1)S(1)} %pad_maximum_fusion.19), channel_id=2, replica_groups=mesh['mp'=4,'latent'=8] {'latent'}, dimensions={0}, use_global_device_ids=true | all-gather | bytes 663552 | tf_op jit(solution)/shard_map/all_gather | solution.py:160
  37.3 9.2 %collective-permute-done.1 = bf16[32,4736]{1,0:T(8,128)(2,1)} collective-permute-done((bf16[32,4736]{1,0:T(8,128)(2,1)}, bf16[32,4736]{1,0:T(8,128)(2,1)}, u32[]{:S(2)}, u32[]{:S(2)}) %collective-permute-start.1) | collective-permute-done | bytes 303136 | tf_op jit(solution)/shard_map/ppermute | solution.py:35
  48.9 2.5 %collective-permute-start.5 = (bf16[32,2304]{1,0:T(8,128)(2,1)S(1)}, bf16[32,2304]{1,0:T(8,128)(2,1)S(1)}, u32[]{:S(2)}, u32[]{:S(2)}) collective-permute-start(bf16[32,2304]{1,0:T(8,128)(2,1)S(1)} %get-tuple-element.59), channel_id=1, source_target_pairs={{0,24},{8,16},{16,8},{24,0},{1,25},{9,17},{17,9},{25,1},{2,26},{10... | collective-permute-start | bytes 442376 | tf_op jit(solution)/shard_map/ppermute | solution.py:35
  51.5 6.7 %collective-permute-start.4 = (bf16[32,2304]{1,0:T(8,128)(2,1)S(1)}, bf16[32,2304]{1,0:T(8,128)(2,1)S(1)}, u32[]{:S(2)}, u32[]{:S(2)}) collective-permute-start(bf16[32,2304]{1,0:T(8,128)(2,1)S(1)} %get-tuple-element.59), channel_id=1, source_target_pairs={{0,16},{8,24},{16,0},{24,8},{1,17},{9,25},{17,1},{25,9},{2,18},{10... | collective-permute-start | bytes 442376 | tf_op jit(solution)/shard_map/ppermute | solution.py:35
  58.4 4.2 %fusion.136 = (bf16[128,2304]{1,0:T(8,128)(2,1)S(1)}, f32[128,2304]{1,0:T(8,128)S(1)}) fusion(bf16[2304,1152]{1,0:T(8,128)(2,1)} %param.19, f32[1152]{0:T(1024)S(1)} %copy-done.3, bf16[32,1152]{1,0:T(8,128)(2,1)S(1)} %get-tuple-element.84, bf16[32,1152]{1,0:T(8,128)(2,1)S(1)} %get-tuple-element.85, bf16[32,1152]{1,0:T(8,128)(2,1)S(1)} %get-tuple-element.86, ...), kind=kOutput, calls=%fused_computation.295 | convolution fusion | flops 681246720 | bytes 7377408 | tf_op jit(solution)/shard_map/dot_general | solution.py:30
  62.7 3.2 %collective-permute-done.4 = bf16[32,2304]{1,0:T(8,128)(2,1)S(1)} collective-permute-done((bf16[32,2304]{1,0:T(8,128)(2,1)S(1)}, bf16[32,2304]{1,0:T(8,128)(2,1)S(1)}, u32[]{:S(2)}, u32[]{:S(2)}) %collective-permute-start.4) | collective-permute-done | bytes 147488 | tf_op jit(solution)/shard_map/ppermute | solution.py:35
  70.5 2.4 %collective-permute-done.7 = bf16[32,1152]{1,0:T(8,128)(2,1)S(1)} collective-permute-done((bf16[32,1152]{1,0:T(8,128)(2,1)S(1)}, bf16[32,1152]{1,0:T(8,128)(2,1)S(1)}, u32[]{:S(2)}, u32[]{:S(2)}) %collective-permute-start.7) | collective-permute-done | bytes 73760 | tf_op jit(solution)/shard_map/ppermute | solution.py:35
  76.3 2.2 %collective-permute-done.10 = bf16[32,1152]{1,0:T(8,128)(2,1)S(1)} collective-permute-done((bf16[32,1152]{1,0:T(8,128)(2,1)S(1)}, bf16[32,1152]{1,0:T(8,128)(2,1)S(1)}, u32[]{:S(2)}, u32[]{:S(2)}) %collective-permute-start.10) | collective-permute-done | bytes 73760 | tf_op jit(solution)/shard_map/ppermute | solution.py:35
  83.1 2.6 %collective-permute-start.14 = (bf16[32,2432]{1,0:T(8,128)(2,1)S(1)}, bf16[32,2432]{1,0:T(8,128)(2,1)S(1)}, u32[]{:S(2)}, u32[]{:S(2)}) collective-permute-start(bf16[32,2432]{1,0:T(8,128)(2,1)S(1)} %get-tuple-element.67), channel_id=1, source_target_pairs={{0,24},{8,16},{16,8},{24,0},{1,25},{9,17},{17,9},{25,1},{2,26},{10... | collective-permute-start | bytes 466952 | tf_op jit(solution)/shard_map/ppermute | solution.py:35
  87.6 2.6 %collective-permute-start.17 = (bf16[32,2304]{1,0:T(8,128)(2,1)S(1)}, bf16[32,2304]{1,0:T(8,128)(2,1)S(1)}, u32[]{:S(2)}, u32[]{:S(2)}) collective-permute-start(bf16[32,2304]{1,0:T(8,128)(2,1)S(1)} %get-tuple-element.73), channel_id=1, source_target_pairs={{0,24},{8,16},{16,8},{24,0},{1,25},{9,17},{17,9},{25,1},{2,26},{10... | collective-permute-start | bytes 442376 | tf_op jit(solution)/shard_map/ppermute | solution.py:35
  92.0 4.2 %collective-permute-start.15 = (bf16[32,2304]{1,0:T(8,128)(2,1)S(1)}, bf16[32,2304]{1,0:T(8,128)(2,1)S(1)}, u32[]{:S(2)}, u32[]{:S(2)}) collective-permute-start(bf16[32,2304]{1,0:T(8,128)(2,1)S(1)} %get-tuple-element.72), channel_id=1, source_target_pairs={{0,8},{8,0},{16,24},{24,16},{1,9},{9,1},{17,25},{25,17},{2,10},{10... | collective-permute-start | bytes 442376 | tf_op jit(solution)/shard_map/ppermute | solution.py:35
  96.2 9.1 %collective-permute-done.13 = bf16[32,2432]{1,0:T(8,128)(2,1)S(1)} collective-permute-done((bf16[32,2432]{1,0:T(8,128)(2,1)S(1)}, bf16[32,2432]{1,0:T(8,128)(2,1)S(1)}, u32[]{:S(2)}, u32[]{:S(2)}) %collective-permute-start.13) | collective-permute-done | bytes 155680 | tf_op jit(solution)/shard_map/ppermute | solution.py:35
  105.5 5.6 %collective-permute-done.16 = bf16[32,2304]{1,0:T(8,128)(2,1)S(1)} collective-permute-done((bf16[32,2304]{1,0:T(8,128)(2,1)S(1)}, bf16[32,2304]{1,0:T(8,128)(2,1)S(1)}, u32[]{:S(2)}, u32[]{:S(2)}) %collective-permute-start.16) | collective-permute-done | bytes 147488 | tf_op jit(solution)/shard_map/ppermute | solution.py:35
  114.0 2.5 %collective-permute-start.18 = (bf16[32,4736]{1,0:T(8,128)(2,1)S(1)}, bf16[32,4736]{1,0:T(8,128)(2,1)S(1)}, u32[]{:S(2)}, u32[]{:S(2)}) collective-permute-start(bf16[32,4736]{1,0:T(8,128)(2,1)S(1)} %pad_maximum_fusion.4), channel_id=1, source_target_pairs={{0,8},{8,0},{16,24},{24,16},{1,9},{9,1},{17,25},{25,17},{2,10},{10... | collective-permute-start | bytes 909320 | tf_op jit(solution)/shard_map/ppermute | solution.py:35
  117.0 7.0 %collective-permute-done.20 = bf16[32,4736]{1,0:T(8,128)(2,1)S(1)} collective-permute-done((bf16[32,4736]{1,0:T(8,128)(2,1)S(1)}, bf16[32,4736]{1,0:T(8,128)(2,1)S(1)}, u32[]{:S(2)}, u32[]{:S(2)}) %collective-permute-start.20) | collective-permute-done | bytes 303136 | tf_op jit(solution)/shard_map/ppermute | solution.py:35
  124.1 15.2 %collective-permute-done.19 = bf16[32,4736]{1,0:T(8,128)(2,1)S(1)} collective-permute-done((bf16[32,4736]{1,0:T(8,128)(2,1)S(1)}, bf16[32,4736]{1,0:T(8,128)(2,1)S(1)}, u32[]{:S(2)}, u32[]{:S(2)}) %collective-permute-start.19) | collective-permute-done | bytes 303136 | tf_op jit(solution)/shard_map/ppermute | solution.py:35
  149.4 2.9 %collective-permute-start.24 = (bf16[32,1024]{1,0:T(8,128)(2,1)S(1)}, bf16[32,1024]{1,0:T(8,128)(2,1)S(1)}, u32[]{:S(2)}, u32[]{:S(2)}) collective-permute-start(bf16[32,1024]{1,0:T(8,128)(2,1)S(1)} %get-tuple-element.94), channel_id=1, source_target_pairs={{0,8},{8,0},{16,24},{24,16},{1,9},{9,1},{17,25},{25,17},{2,10},{10... | collective-permute-start | bytes 196616 | tf_op jit(solution)/shard_map/ppermute | solution.py:35
  155.0 2.3 %collective-permute-done.32 = bf16[32,1280]{1,0:T(8,128)(2,1)S(1)} collective-permute-done((bf16[32,1280]{1,0:T(8,128)(2,1)S(1)}, bf16[32,1280]{1,0:T(8,128)(2,1)S(1)}, u32[]{:S(2)}, u32[]{:S(2)}) %collective-permute-start.32) | collective-permute-done | bytes 81952 | tf_op jit(solution)/shard_map/ppermute | solution.py:35
  159.1 3.0 %collective-permute-start.21 = (bf16[32,1024]{1,0:T(8,128)(2,1)S(1)}, bf16[32,1024]{1,0:T(8,128)(2,1)S(1)}, u32[]{:S(2)}, u32[]{:S(2)}) collective-permute-start(bf16[32,1024]{1,0:T(8,128)(2,1)S(1)} %get-tuple-element.91), channel_id=1, source_target_pairs={{0,8},{8,0},{16,24},{24,16},{1,9},{9,1},{17,25},{25,17},{2,10},{10... | collective-permute-start | bytes 196616 | tf_op jit(solution)/shard_map/ppermute | solution.py:35
  174.9 3.2 %collective-permute-done.36 = f32[9,1024]{1,0:T(8,128)S(1)} collective-permute-done((f32[9,1024]{1,0:T(8,128)S(1)}, f32[9,1024]{1,0:T(8,128)S(1)}, u32[]{:S(2)}, u32[]{:S(2)}) %collective-permute-start.36) | collective-permute-done | bytes 36896 | tf_op jit(solution)/shard_map/ppermute | solution.py:35
  180.0 4.1 %collective-permute-done.37 = f32[9,1024]{1,0:T(8,128)S(1)} collective-permute-done((f32[9,1024]{1,0:T(8,128)S(1)}, f32[9,1024]{1,0:T(8,128)S(1)}, u32[]{:S(2)}, u32[]{:S(2)}) %collective-permute-start.37) | collective-permute-done | bytes 36896 | tf_op jit(solution)/shard_map/ppermute | solution.py:35
  (225 shorter events, 60.7 us)
Async XLA Ops:
  20.5 16.7 %collective-permute-start = (bf16[32,4736]{1,0:T(8,128)(2,1)}, bf16[32,4736]{1,0:T(8,128)(2,1)S(1)}, u32[]{:S(2)}, u32[]{:S(2)}) collective-permute-start(bf16[32,4736]{1,0:T(8,128)(2,1)} %get-tuple-element.64), channel_id=1, source_target_pairs={{0,8},{8,0},{16,24},{24,16},{1,9},{9,1},{17,25},{25,17},{2,10},{10... | collective-permute-start | bytes 909320 | tf_op jit(solution)/shard_map/ppermute | solution.py:35
  22.1 24.3 %collective-permute-start.1 = (bf16[32,4736]{1,0:T(8,128)(2,1)}, bf16[32,4736]{1,0:T(8,128)(2,1)}, u32[]{:S(2)}, u32[]{:S(2)}) collective-permute-start(bf16[32,4736]{1,0:T(8,128)(2,1)} %get-tuple-element.63), channel_id=1, source_target_pairs={{0,16},{8,24},{16,0},{24,8},{1,17},{9,25},{17,1},{25,9},{2,18},{10... | collective-permute-start | bytes 909320 | tf_op jit(solution)/shard_map/ppermute | solution.py:35
  24.7 21.7 %collective-permute-start.2 = (bf16[32,4736]{1,0:T(8,128)(2,1)}, bf16[32,4736]{1,0:T(8,128)(2,1)}, u32[]{:S(2)}, u32[]{:S(2)}) collective-permute-start(bf16[32,4736]{1,0:T(8,128)(2,1)} %get-tuple-element.62), channel_id=1, source_target_pairs={{0,24},{8,16},{16,8},{24,0},{1,25},{9,17},{17,9},{25,1},{2,26},{10... | collective-permute-start | bytes 909320 | tf_op jit(solution)/shard_map/ppermute | solution.py:35
  48.9 13.7 %collective-permute-start.5 = (bf16[32,2304]{1,0:T(8,128)(2,1)S(1)}, bf16[32,2304]{1,0:T(8,128)(2,1)S(1)}, u32[]{:S(2)}, u32[]{:S(2)}) collective-permute-start(bf16[32,2304]{1,0:T(8,128)(2,1)S(1)} %get-tuple-element.59), channel_id=1, source_target_pairs={{0,24},{8,16},{16,8},{24,0},{1,25},{9,17},{17,9},{25,1},{2,26},{10... | collective-permute-start | bytes 442376 | tf_op jit(solution)/shard_map/ppermute | solution.py:35
  51.5 14.4 %collective-permute-start.4 = (bf16[32,2304]{1,0:T(8,128)(2,1)S(1)}, bf16[32,2304]{1,0:T(8,128)(2,1)S(1)}, u32[]{:S(2)}, u32[]{:S(2)}) collective-permute-start(bf16[32,2304]{1,0:T(8,128)(2,1)S(1)} %get-tuple-element.59), channel_id=1, source_target_pairs={{0,16},{8,24},{16,0},{24,8},{1,17},{9,25},{17,1},{25,9},{2,18},{10... | collective-permute-start | bytes 442376 | tf_op jit(solution)/shard_map/ppermute | solution.py:35
  58.2 7.7 %collective-permute-start.3 = (bf16[32,2304]{1,0:T(8,128)(2,1)S(1)}, bf16[32,2304]{1,0:T(8,128)(2,1)S(1)}, u32[]{:S(2)}, u32[]{:S(2)}) collective-permute-start(bf16[32,2304]{1,0:T(8,128)(2,1)S(1)} %get-tuple-element.59), channel_id=1, source_target_pairs={{0,8},{8,0},{16,24},{24,16},{1,9},{9,1},{17,25},{25,17},{2,10},{10... | collective-permute-start | bytes 442376 | tf_op jit(solution)/shard_map/ppermute | solution.py:35
  83.1 8.9 %collective-permute-start.14 = (bf16[32,2432]{1,0:T(8,128)(2,1)S(1)}, bf16[32,2432]{1,0:T(8,128)(2,1)S(1)}, u32[]{:S(2)}, u32[]{:S(2)}) collective-permute-start(bf16[32,2432]{1,0:T(8,128)(2,1)S(1)} %get-tuple-element.67), channel_id=1, source_target_pairs={{0,24},{8,16},{16,8},{24,0},{1,25},{9,17},{17,9},{25,1},{2,26},{10... | collective-permute-start | bytes 466952 | tf_op jit(solution)/shard_map/ppermute | solution.py:35
  85.7 19.6 %collective-permute-start.13 = (bf16[32,2432]{1,0:T(8,128)(2,1)S(1)}, bf16[32,2432]{1,0:T(8,128)(2,1)S(1)}, u32[]{:S(2)}, u32[]{:S(2)}) collective-permute-start(bf16[32,2432]{1,0:T(8,128)(2,1)S(1)} %get-tuple-element.66), channel_id=1, source_target_pairs={{0,16},{8,24},{16,0},{24,8},{1,17},{9,25},{17,1},{25,9},{2,18},{10... | collective-permute-start | bytes 466952 | tf_op jit(solution)/shard_map/ppermute | solution.py:35
  85.7 19.6 %collective-permute-start.12 = (bf16[32,2432]{1,0:T(8,128)(2,1)S(1)}, bf16[32,2432]{1,0:T(8,128)(2,1)S(1)}, u32[]{:S(2)}, u32[]{:S(2)}) collective-permute-start(bf16[32,2432]{1,0:T(8,128)(2,1)S(1)} %get-tuple-element.65), channel_id=1, source_target_pairs={{0,8},{8,0},{16,24},{24,16},{1,9},{9,1},{17,25},{25,17},{2,10},{10... | collective-permute-start | bytes 466952 | tf_op jit(solution)/shard_map/ppermute | solution.py:35
  87.6 17.9 %collective-permute-start.17 = (bf16[32,2304]{1,0:T(8,128)(2,1)S(1)}, bf16[32,2304]{1,0:T(8,128)(2,1)S(1)}, u32[]{:S(2)}, u32[]{:S(2)}) collective-permute-start(bf16[32,2304]{1,0:T(8,128)(2,1)S(1)} %get-tuple-element.73), channel_id=1, source_target_pairs={{0,24},{8,16},{16,8},{24,0},{1,25},{9,17},{17,9},{25,1},{2,26},{10... | collective-permute-start | bytes 442376 | tf_op jit(solution)/shard_map/ppermute | solution.py:35
  90.2 20.9 %collective-permute-start.16 = (bf16[32,2304]{1,0:T(8,128)(2,1)S(1)}, bf16[32,2304]{1,0:T(8,128)(2,1)S(1)}, u32[]{:S(2)}, u32[]{:S(2)}) collective-permute-start(bf16[32,2304]{1,0:T(8,128)(2,1)S(1)} %get-tuple-element.74), channel_id=1, source_target_pairs={{0,16},{8,24},{16,0},{24,8},{1,17},{9,25},{17,1},{25,9},{2,18},{10... | collective-permute-start | bytes 442376 | tf_op jit(solution)/shard_map/ppermute | solution.py:35
  92.0 19.1 %collective-permute-start.15 = (bf16[32,2304]{1,0:T(8,128)(2,1)S(1)}, bf16[32,2304]{1,0:T(8,128)(2,1)S(1)}, u32[]{:S(2)}, u32[]{:S(2)}) collective-permute-start(bf16[32,2304]{1,0:T(8,128)(2,1)S(1)} %get-tuple-element.72), channel_id=1, source_target_pairs={{0,8},{8,0},{16,24},{24,16},{1,9},{9,1},{17,25},{25,17},{2,10},{10... | collective-permute-start | bytes 442376 | tf_op jit(solution)/shard_map/ppermute | solution.py:35
  112.0 12.0 %collective-permute-start.20 = (bf16[32,4736]{1,0:T(8,128)(2,1)S(1)}, bf16[32,4736]{1,0:T(8,128)(2,1)S(1)}, u32[]{:S(2)}, u32[]{:S(2)}) collective-permute-start(bf16[32,4736]{1,0:T(8,128)(2,1)S(1)} %pad_maximum_fusion.4), channel_id=1, source_target_pairs={{0,24},{8,16},{16,8},{24,0},{1,25},{9,17},{17,9},{25,1},{2,26},{10... | collective-permute-start | bytes 909320 | tf_op jit(solution)/shard_map/ppermute | solution.py:35
  114.0 25.3 %collective-permute-start.19 = (bf16[32,4736]{1,0:T(8,128)(2,1)S(1)}, bf16[32,4736]{1,0:T(8,128)(2,1)S(1)}, u32[]{:S(2)}, u32[]{:S(2)}) collective-permute-start(bf16[32,4736]{1,0:T(8,128)(2,1)S(1)} %pad_maximum_fusion.4), channel_id=1, source_target_pairs={{0,16},{8,24},{16,0},{24,8},{1,17},{9,25},{17,1},{25,9},{2,18},{10... | collective-permute-start | bytes 909320 | tf_op jit(solution)/shard_map/ppermute | solution.py:35
  114.0 25.3 %collective-permute-start.18 = (bf16[32,4736]{1,0:T(8,128)(2,1)S(1)}, bf16[32,4736]{1,0:T(8,128)(2,1)S(1)}, u32[]{:S(2)}, u32[]{:S(2)}) collective-permute-start(bf16[32,4736]{1,0:T(8,128)(2,1)S(1)} %pad_maximum_fusion.4), channel_id=1, source_target_pairs={{0,8},{8,0},{16,24},{24,16},{1,9},{9,1},{17,25},{25,17},{2,10},{10... | collective-permute-start | bytes 909320 | tf_op jit(solution)/shard_map/ppermute | solution.py:35
  145.8 6.6 %collective-permute-start.31 = (bf16[32,1280]{1,0:T(8,128)(2,1)S(1)}, bf16[32,1280]{1,0:T(8,128)(2,1)S(1)}, u32[]{:S(2)}, u32[]{:S(2)}) collective-permute-start(bf16[32,1280]{1,0:T(8,128)(2,1)S(1)} %pad_maximum_fusion.15), channel_id=1, source_target_pairs={{0,2},{1,3},{2,0},{3,1},{4,6},{5,7},{6,4},{7,5},{8,10},{9,11},{10,... | collective-permute-start | bytes 245768 | tf_op jit(solution)/shard_map/ppermute | solution.py:35
  147.9 11.2 %collective-permute-start.26 = (bf16[32,1024]{1,0:T(8,128)(2,1)S(1)}, bf16[32,1024]{1,0:T(8,128)(2,1)S(1)}, u32[]{:S(2)}, u32[]{:S(2)}) collective-permute-start(bf16[32,1024]{1,0:T(8,128)(2,1)S(1)} %get-tuple-element.95), channel_id=1, source_target_pairs={{0,24},{8,16},{16,8},{24,0},{1,25},{9,17},{17,9},{25,1},{2,26},{10... | collective-permute-start | bytes 196616 | tf_op jit(solution)/shard_map/ppermute | solution.py:35
  149.4 12.7 %collective-permute-start.25 = (bf16[32,1024]{1,0:T(8,128)(2,1)S(1)}, bf16[32,1024]{1,0:T(8,128)(2,1)S(1)}, u32[]{:S(2)}, u32[]{:S(2)}) collective-permute-start(bf16[32,1024]{1,0:T(8,128)(2,1)S(1)} %get-tuple-element.96), channel_id=1, source_target_pairs={{0,16},{8,24},{16,0},{24,8},{1,17},{9,25},{17,1},{25,9},{2,18},{10... | collective-permute-start | bytes 196616 | tf_op jit(solution)/shard_map/ppermute | solution.py:35
  149.4 12.8 %collective-permute-start.24 = (bf16[32,1024]{1,0:T(8,128)(2,1)S(1)}, bf16[32,1024]{1,0:T(8,128)(2,1)S(1)}, u32[]{:S(2)}, u32[]{:S(2)}) collective-permute-start(bf16[32,1024]{1,0:T(8,128)(2,1)S(1)} %get-tuple-element.94), channel_id=1, source_target_pairs={{0,8},{8,0},{16,24},{24,16},{1,9},{9,1},{17,25},{25,17},{2,10},{10... | collective-permute-start | bytes 196616 | tf_op jit(solution)/shard_map/ppermute | solution.py:35
  157.3 6.1 %collective-permute-start.23 = (bf16[32,1024]{1,0:T(8,128)(2,1)S(1)}, bf16[32,1024]{1,0:T(8,128)(2,1)S(1)}, u32[]{:S(2)}, u32[]{:S(2)}) collective-permute-start(bf16[32,1024]{1,0:T(8,128)(2,1)S(1)} %get-tuple-element.92), channel_id=1, source_target_pairs={{0,24},{8,16},{16,8},{24,0},{1,25},{9,17},{17,9},{25,1},{2,26},{10... | collective-permute-start | bytes 196616 | tf_op jit(solution)/shard_map/ppermute | solution.py:35
  158.7 6.1 %collective-permute-start.22 = (bf16[32,1024]{1,0:T(8,128)(2,1)S(1)}, bf16[32,1024]{1,0:T(8,128)(2,1)S(1)}, u32[]{:S(2)}, u32[]{:S(2)}) collective-permute-start(bf16[32,1024]{1,0:T(8,128)(2,1)S(1)} %get-tuple-element.93), channel_id=1, source_target_pairs={{0,16},{8,24},{16,0},{24,8},{1,17},{9,25},{17,1},{25,9},{2,18},{10... | collective-permute-start | bytes 196616 | tf_op jit(solution)/shard_map/ppermute | solution.py:35
  162.1 7.4 %collective-permute-start.35 = (bf16[64,1280]{1,0:T(8,128)(2,1)S(1)}, bf16[64,1280]{1,0:T(8,128)(2,1)S(1)}, u32[]{:S(2)}, u32[]{:S(2)}) collective-permute-start(bf16[64,1280]{1,0:T(8,128)(2,1)S(1)} %pad_maximum_fusion.8), channel_id=1, source_target_pairs={{0,1},{1,0},{2,3},{3,2},{4,5},{5,4},{6,7},{7,6},{8,9},{9,8},{10,11... | collective-permute-start | bytes 491528 | tf_op jit(solution)/shard_map/ppermute | solution.py:35
  165.1 6.1 %collective-permute-start.29 = (bf16[32,1024]{1,0:T(8,128)(2,1)S(1)}, bf16[32,1024]{1,0:T(8,128)(2,1)S(1)}, u32[]{:S(2)}, u32[]{:S(2)}) collective-permute-start(bf16[32,1024]{1,0:T(8,128)(2,1)S(1)} %fusion.74), channel_id=1, source_target_pairs={{0,24},{8,16},{16,8},{24,0},{1,25},{9,17},{17,9},{25,1},{2,26},{10... | collective-permute-start | bytes 196616 | tf_op jit(solution)/shard_map/ppermute | solution.py:35
  178.1 5.9 %collective-permute-start.37 = (f32[9,1024]{1,0:T(8,128)S(1)}, f32[9,1024]{1,0:T(8,128)S(1)}, u32[]{:S(2)}, u32[]{:S(2)}) collective-permute-start(f32[9,1024]{1,0:T(8,128)S(1)} %add.355), channel_id=1, source_target_pairs={{0,16},{8,24},{16,0},{24,8},{1,17},{9,25},{17,1},{25,9},{2,18},{10... | collective-permute-start | bytes 110600 | tf_op jit(solution)/shard_map/ppermute | solution.py:35
  (46 other events, 538.1 us)

commit v2 on v1

v2 whole, which is shorter than its diff:
```python
import jax
import jax.numpy as jnp
from jax import lax
from jax.sharding import PartitionSpec as P


epsilon = 1e-06
tanh_scale = 0.7978845608028654
cubic_term = 0.044715
LANES = 128
f32 = jnp.float32
bf16 = jnp.bfloat16


def gelu_parts(gate_sum):
    inner = tanh_scale * (gate_sum + cubic_term * gate_sum * gate_sum * gate_sum)
    tangent = jnp.tanh(inner)
    gelu_value = 0.5 * gate_sum * (1.0 + tangent)
    gelu_slope = 0.5 * (1.0 + tangent) + 0.5 * gate_sum * (1.0 - tangent * tangent) * tanh_scale * (
        1.0 + 3.0 * cubic_term * gate_sum * gate_sum
    )
    return (gelu_value, gelu_slope)


def dot(left, right):
    return jnp.dot(left, right, preferred_element_type=f32)


def dot_transposed(left, right):
    return lax.dot_general(left, right, (((1,), (1,)), ((), ())), preferred_element_type=f32)


def swap(value, axis, distance):
    count = lax.axis_size(axis)
    return lax.ppermute(value, axis, [(i, i ^ distance) for i in range(count)])


def split_columns(columns):
    rows = columns[0].shape[0]
    lane = lax.broadcasted_iota(jnp.int32, (rows, LANES), 1)
    block = jnp.zeros((rows, LANES), f32)
    for index, column in enumerate(columns):
        high = lax.reduce_precision(column, 8, 7)
        rest = column - high
        middle = lax.reduce_precision(rest, 8, 7)
        for part, piece in enumerate((high, middle, rest - middle)):
            block = jnp.where(lane == 3 * index + part, piece, block)
    return block.astype(bf16)


def join_columns(block, count):
    lane = lax.broadcasted_iota(jnp.int32, block.shape, 1)
    wide = block.astype(f32)
    return [
        jnp.sum(jnp.where(lane // 3 == index, wide, 0.0), axis=1, keepdims=True)
        for index in range(count)
    ]


def send_mp(blocks):
    got = []
    for m in reversed(range(1, lax.axis_size("mp"))):
        got.append(swap(blocks[m - 1], "mp", m))
    return got


def gather_mp(block):
    blocks = [block]
    for m in reversed(range(1, lax.axis_size("mp"))):
        blocks.insert(1, swap(block, "mp", m))
    return jnp.concatenate(blocks, axis=0)


def reduce_latent(partial, extra, side):
    count = lax.axis_size("latent")
    half = partial.shape[0] // 2
    width = partial.shape[1]

    def pack(main, column):
        return main if column is None else jnp.concatenate([main, split_columns([column])], axis=1)

    def add(main, column, got):
        total = (main.astype(f32) + got[:, :width].astype(f32)).astype(bf16)
        return total, None if column is None else column + join_columns(got[:, width:], 1)[0]

    def pick(value, first):
        return jnp.where(first, value[:half], value[half:])

    main, column = pick(partial, side), None if extra is None else pick(extra, side)
    sent = pack(pick(partial, ~side), None if extra is None else pick(extra, ~side))
    got = swap(sent, "latent", 1)
    main, column = add(main, column, got)
    distances = [1 << bit for bit in range(1, count.bit_length() - 1)]
    quarter = half // 2
    done = []
    for lower, order in ((0, distances), (quarter, distances[::-1])):
        done.append(
            [main[lower : lower + quarter], None if column is None else column[lower : lower + quarter], order]
        )
    for step in range(len(distances)):
        got = [swap(pack(m, c), "latent", order[step]) for m, c, order in done]
        done = [[*add(m, c, g), order] for (m, c, order), g in zip(done, got)]
    main = jnp.concatenate([d[0] for d in done], axis=0)
    column = None if extra is None else jnp.concatenate([d[1] for d in done], axis=0)
    other = swap(pack(main, column), "latent", 1)
    low = jnp.where(side, main, other[:, :width])
    high = jnp.where(side, other[:, :width], main)
    total = jnp.concatenate([low, high], axis=0)
    if extra is None:
        return total, None
    far = join_columns(other[:, width:], 1)[0]
    return total, jnp.concatenate([jnp.where(side, column, far), jnp.where(side, far, column)], axis=0)


def program(
    clean_stream,
    patch_stream,
    output_grad,
    input_gain,
    gate_weight,
    up_weight,
    down_weight,
    output_gain,
    encoder_weight,
    encoder_bias,
    decoder_weight,
    decoder_bias,
    patch_positions,
):
    mp_count = lax.axis_size("mp")
    mp_index = lax.axis_index("mp")
    latent_index = lax.axis_index("latent")
    local_rows = clean_stream.shape[0]
    model_width = clean_stream.shape[1] * mp_count
    hidden_width = gate_weight.shape[1]
    tokens = local_rows * lax.axis_size("latent")
    rows = tokens // mp_count

    def total(own, pieces):
        for piece in pieces:
            own = own + piece.astype(f32)
        return own

    sequences, picks = patch_positions.shape
    length = tokens // sequences
    starts = [(mp_index ^ m) * rows for m in range(mp_count)]
    side = (latent_index & 1) == 0
    own_row = latent_index * local_rows
    own_row = (mp_index ^ lax.div(own_row, rows)) * rows + lax.rem(own_row, rows)
    streams = jnp.concatenate([clean_stream, output_grad, patch_stream], axis=1)
    starts, side, own_row, mp_index, streams = lax.optimization_barrier(
        (starts, side, own_row, mp_index, streams)
    )

    def block_of(value, distance):
        zero = jnp.zeros((), jnp.int32)
        return lax.dynamic_slice(
            value, (starts[distance], zero), (rows, value.shape[1]), allow_negative_indices=False
        )

    def blocks_of(value):
        return [block_of(value, m) for m in range(1, mp_count)]

    streams = lax.all_gather(streams, "latent", axis=0, tiled=True)
    width = clean_stream.shape[1]
    clean = streams[:, :width]
    clean_rows = clean.astype(f32)
    scaled = (clean_rows * input_gain).astype(bf16)
    gate_part = dot(scaled, gate_weight)
    square_part = jnp.sum(clean_rows * clean_rows, axis=1, keepdims=True)
    gate_sent = jnp.concatenate([gate_part.astype(bf16), split_columns([square_part])], axis=1)
    gate_got = send_mp(blocks_of(gate_sent))
    up_part = dot(scaled, up_weight)
    up_sent = up_part.astype(bf16)
    up_got = send_mp(blocks_of(up_sent))
    streams, patch_positions, mp_index, _ = lax.optimization_barrier(
        (streams, patch_positions, mp_index, up_sent)
    )
    place = jnp.arange(tokens, dtype=jnp.int32)
    token = (mp_index ^ lax.div(place, rows)) * rows + lax.rem(place, rows)
    targets = patch_positions + jnp.arange(sequences, dtype=jnp.int32)[:, None] * length
    inside = lax.div(token, length)[None] == jnp.arange(sequences, dtype=jnp.int32)[:, None]
    chosen = jnp.concatenate([inside, targets.reshape(-1, 1) == token[None]], axis=0).astype(f32)
    grad, patch = streams[:, width : 2 * width], streams[:, 2 * width :]

    square_in = block_of(square_part, 0)
    for piece in gate_got:
        square_in = square_in + join_columns(piece[:, hidden_width:], 1)[0]
    in_scale = lax.rsqrt(square_in / model_width + epsilon)
    gate_sum = total(block_of(gate_part, 0), [piece[:, :hidden_width] for piece in gate_got]) * in_scale
    up_sum = total(block_of(up_part, 0), up_got) * in_scale
    hidden = (gelu_parts(gate_sum)[0] * up_sum).astype(bf16)
    hidden_all = gather_mp(hidden)
    gate_sum, up_sum, _ = lax.optimization_barrier((gate_sum, up_sum, hidden))
    gelu_value, gelu_slope = gelu_parts(gate_sum)
    gate_factor = up_sum * gelu_slope
    radial = gate_factor * gate_sum + gelu_value * up_sum

    linear_part = dot_transposed((output_gain * grad.astype(f32)).astype(bf16), down_weight)
    linear_sent = linear_part.astype(bf16)
    linear_got = send_mp(blocks_of(linear_sent))

    encode_clean = dot((clean_rows - decoder_bias).astype(bf16), encoder_weight)
    encode_patch = dot((patch.astype(f32) - decoder_bias).astype(bf16), encoder_weight)
    encode_sent = [
        jnp.concatenate([block_of(encode_clean, m), block_of(encode_patch, m)], axis=0).astype(bf16)
        for m in range(1, mp_count)
    ]

    ordered = [jnp.concatenate([block_of(v, m) for m in range(mp_count)], axis=0) for v in (clean, grad)]
    clean_rows, grad_rows = (value.astype(f32) for value in lax.optimization_barrier(ordered))
    weighted_out = output_gain * grad_rows

    mlp_part = dot(hidden_all, down_weight).astype(bf16)
    mlp_out, _ = reduce_latent(mlp_part, None, side)
    mlp_rows = mlp_out.astype(f32)
    square_out = jnp.sum(mlp_rows * mlp_rows, axis=1, keepdims=True)
    cross_out = jnp.sum(mlp_rows * weighted_out, axis=1, keepdims=True)
    back_part = dot_transposed(mlp_out, down_weight)
    back_sent = jnp.concatenate([back_part.astype(bf16), split_columns([square_out, cross_out])], axis=1)
    back_got = send_mp([back_sent[m * rows : (m + 1) * rows] for m in range(1, mp_count)])
    square_own, cross_own = square_out[:rows], cross_out[:rows]
    for piece in back_got:
        square_piece, cross_piece = join_columns(piece[:, hidden_width:], 2)
        square_own, cross_own = square_own + square_piece, cross_own + cross_piece
    out_scale = lax.rsqrt(square_own / model_width + epsilon)
    hidden_grad = out_scale * total(block_of(linear_part, 0), linear_got) - (
        out_scale * out_scale * out_scale * (cross_own / model_width)
    ) * total(back_part[:rows], [piece[:, :hidden_width] for piece in back_got])
    gate_grad = (hidden_grad * gate_factor).astype(bf16)
    cross_in = jnp.sum(hidden_grad * radial, axis=1, keepdims=True)
    gate_grads = gather_mp(jnp.concatenate([gate_grad, split_columns([cross_in, in_scale, out_scale])], axis=1))
    up_grads = gather_mp((hidden_grad * gelu_value).astype(bf16))
    cross_in, in_scale, out_scale = join_columns(gate_grads[:, hidden_width:], 3)


    encode_got = send_mp(encode_sent)
    latents = encoder_weight.shape[1]
    own_sums = jnp.concatenate([block_of(encode_clean, 0), block_of(encode_patch, 0)], axis=0)
    feature = jnp.maximum(total(own_sums, encode_got) + encoder_bias, 0.0)
    feature_delta = gather_mp((feature[rows:] - feature[:rows]).astype(bf16)).astype(f32)

    gate_back = dot_transposed(gate_grads[:, :hidden_width], gate_weight)
    normed_part = dot_transposed(up_grads, up_weight) + gate_back
    normed_grad, cross_in = reduce_latent(normed_part.astype(bf16), cross_in, side)
    site_grad = (
        grad_rows
        + in_scale * (input_gain * normed_grad.astype(f32))
        - clean_rows * (in_scale * in_scale * (cross_in / model_width))
    ).astype(bf16)
    contribution = feature_delta * dot_transposed(site_grad, decoder_weight)

    effects = jnp.dot(chosen, contribution, precision=lax.Precision.HIGHEST)
    mlp_out, out_scale, effects = lax.optimization_barrier((mlp_out, out_scale, effects))

    def own(value):
        zero = jnp.zeros((), jnp.int32)
        return lax.dynamic_slice(
            value, (own_row, zero), (local_rows, value.shape[1]), allow_negative_indices=False
        )

    block_rows = (
        clean_stream.astype(f32) + own(mlp_out).astype(f32) * own(out_scale) * output_gain
    ).astype(bf16)
    terms = [effects] + [swap(effects, "mp", m) for m in range(1, mp_count)]
    while len(terms) > 1:
        terms = [left + right for left, right in zip(terms[::2], terms[1::2])]
    effects = terms[0]
    return (block_rows, effects[:sequences], effects[sequences:].reshape(sequences, picks, latents))


def solution(mesh):
    in_specs = (
        P("latent", "mp"),
        P("latent", "mp"),
        P("latent", "mp"),
        P("mp"),
        P("mp", "latent"),
        P("mp", "latent"),
        P("latent", "mp"),
        P("mp"),
        P("mp", "latent"),
        P("latent"),
        P("latent", "mp"),
        P("mp"),
        P(),
    )
    out_specs = (P("latent", "mp"), P(None, "latent"), P(None, None, "latent"))
    return jax.shard_map(program, mesh=mesh, in_specs=in_specs, out_specs=out_specs, check_vma=False)
```

time: 186 us -> 180 us (0.968)
  blocking collectives: 21.2 us -> 12.4 us
  local copies, waits for them, and re-layouts: 2.63 us -> 8.95 us
  waiting for transfers between devices: 76.5 us -> 70.7 us
  other arithmetic: 10.2 us -> 13.5 us
    all_gather x2 -> x1, blocking collectives: 21.2 us -> 12.4 us  [program(): streams = lax.all_gather(streams, 'latent', axis=0, tiled=True)]
    ppermute x38 -> x42, waiting for transfers between devices: 76.5 us -> 70.7 us  [swap(): return lax.ppermute(value, axis, [(i, i ^ distance) for i in range(count)])]
    dynamic_slice x3 -> x6, local copies, waits for them, and re-layouts: 0.09 us -> 3.77 us  [block_of(): lax.dynamic_slice(value, (starts[distance], zero), (rows, value.shape[1])...]
    concatenate x5 -> x8, other arithmetic: 0.24 us -> 3.57 us  [the longest x3 1.61 us: program(): jnp.concatenate([block_of(encode_clean, m), block_of(encode_patch, m)], a...]
    dot_general x5, matrix products: 8.63 us -> 11 us  [dot(): return jnp.dot(left, right, preferred_element_type=f32)]
    unnamed x64 -> x72, local copies, waits for them, and re-layouts: 0.17 us -> 2.42 us
    ppermute x38 -> x42, starting transfers between devices: 53.9 us -> 52.3 us  [swap(): return lax.ppermute(value, axis, [(i, i ^ distance) for i in range(count)])]
  transfers between devices with their start and end apart: 38 -> 42, of which waited for: 23 -> 22; matrix products, arithmetic and copies ran while one was open for 6% -> 18% of each run, Pallas kernels for 0% -> 0%
where the time goes in v2:
time: 180 us
  waiting for transfers between devices  70.7 us (39%)
  starting transfers between devices  52.3 us (29%)
  matrix products  20.2 us (11%)
  other arithmetic  13.5 us (8%)
  blocking collectives  12.4 us (7%)
  local copies, waits for them, and re-layouts  8.95 us (5%)
    ppermute x42, waiting for transfers between devices, swap(): return lax.ppermute(value, axis, [(i, i ^ distance) for i in range(count)])  70.7 us
    ppermute x42, starting transfers between devices, swap(): return lax.ppermute(value, axis, [(i, i ^ distance) for i in range(count)])  52.3 us
    all_gather x1, blocking collectives, program(): streams = lax.all_gather(streams, 'latent', axis=0, tiled=True)  12.4 us
    dot_general x5, matrix products, dot(): return jnp.dot(left, right, preferred_element_type=f32)  11 us
    dot_general x5, matrix products, dot_transposed(): lax.dot_general(left, right, (((1,), (1,)), ((), ())), preferred_element_...  8.79 us
    dynamic_slice x6, local copies, waits for them, and re-layouts, block_of(): lax.dynamic_slice(value, (starts[distance], zero), (rows, value.shape[1])...  3.77 us
  transfers between devices with their start and end apart: 42, of which 22 were waited for; matrix products, arithmetic and copies ran while one was open for 18% of the time, Pallas kernels for 0%

profile of v2, /device:TPU:0, one launch (start us, length us, event | category | flops | bytes accessed | tf_op | source)
XLA Modules:
  0.0 179.7 jit_solution(14272288078212337067)
XLA Ops:
  1.7 12.4 %all_gather.3 = bf16[128,3456]{1,0:T(8,128)(2,1)S(1)} all-gather(bf16[16,3456]{1,0:T(8,128)(2,1)S(1)} %pad_maximum_fusion.22), channel_id=1, replica_groups=mesh['mp'=4,'latent'=8] {'latent'}, dimensions={0}, use_global_device_ids=true | all-gather | bytes 995328 | tf_op jit(solution)/shard_map/all_gather | solution.py:164
  14.9 4.6 %fusion.126 = (bf16[128,2304]{1,0:T(8,128)(2,1)S(1)}, f32[128,2304]{1,0:T(8,128)}) fusion(bf16[1152,2304]{1,0:T(8,128)(2,1)} %param.17, f32[1152]{0:T(1024)} %param.16, bf16[128,3456]{1,0:T(8,128)(2,1)S(1)} %all_gather.3), kind=kOutput, calls=%fused_computation.297 | convolution fusion | flops 680214528 | bytes 7377408 | tf_op jit(solution)/shard_map/dot_general | solution.py:26
  20.6 2.6 %collective-permute-start.1 = (bf16[32,2432]{1,0:T(8,128)(2,1)}, bf16[32,2432]{1,0:T(8,128)(2,1)}, u32[]{:S(2)}, u32[]{:S(2)}) collective-permute-start(bf16[32,2432]{1,0:T(8,128)(2,1)} %get-tuple-element.83), channel_id=1, source_target_pairs={{0,16},{8,24},{16,0},{24,8},{1,17},{9,25},{17,1},{25,9},{2,18},{10... | collective-permute-start | bytes 466952 | tf_op jit(solution)/shard_map/ppermute | solution.py:35
  27.6 2.9 %collective-permute-start.3 = (bf16[32,2304]{1,0:T(8,128)(2,1)}, bf16[32,2304]{1,0:T(8,128)(2,1)}, u32[]{:S(2)}, u32[]{:S(2)}) collective-permute-start(bf16[32,2304]{1,0:T(8,128)(2,1)} %get-tuple-element.89), channel_id=1, source_target_pairs={{0,24},{8,16},{16,8},{24,0},{1,25},{9,17},{17,9},{25,1},{2,26},{10... | collective-permute-start | bytes 442376 | tf_op jit(solution)/shard_map/ppermute | solution.py:35
  35.6 2.6 %fusion.129 = (bf16[128,2304]{1,0:T(8,128)(2,1)S(1)}, f32[128,2304]{1,0:T(8,128)}) fusion(bf16[2304,1152]{1,0:T(8,128)(2,1)S(1)} %bitcast.17, f32[1152]{0:T(1024)S(1)} %copy-done.11, bf16[128,3456]{1,0:T(8,128)(2,1)S(1)} %all_gather.3), kind=kOutput, calls=%fused_computation.300 | convolution fusion | flops 680214528 | bytes 7380992 | tf_op jit(solution)/shard_map/dot_general | solution.py:30
  47.5 6.8 %collective-permute-done.4 = bf16[32,2304]{1,0:T(8,128)(2,1)S(1)} collective-permute-done((bf16[32,2304]{1,0:T(8,128)(2,1)}, bf16[32,2304]{1,0:T(8,128)(2,1)S(1)}, u32[]{:S(2)}, u32[]{:S(2)}) %collective-permute-start.4) | collective-permute-done | bytes 147488 | tf_op jit(solution)/shard_map/ppermute | solution.py:35
  56.0 2.7 %collective-permute-start.8 = (bf16[32,2304]{1,0:T(8,128)(2,1)S(1)}, bf16[32,2304]{1,0:T(8,128)(2,1)S(1)}, u32[]{:S(2)}, u32[]{:S(2)}) collective-permute-start(bf16[32,2304]{1,0:T(8,128)(2,1)S(1)} %get-tuple-element.75), channel_id=1, source_target_pairs={{0,24},{8,16},{16,8},{24,0},{1,25},{9,17},{17,9},{25,1},{2,26},{10... | collective-permute-start | bytes 442376 | tf_op jit(solution)/shard_map/ppermute | solution.py:35
  60.5 4.0 %collective-permute-done.8 = bf16[32,2304]{1,0:T(8,128)(2,1)S(1)} collective-permute-done((bf16[32,2304]{1,0:T(8,128)(2,1)S(1)}, bf16[32,2304]{1,0:T(8,128)(2,1)S(1)}, u32[]{:S(2)}, u32[]{:S(2)}) %collective-permute-start.8) | collective-permute-done | bytes 147488 | tf_op jit(solution)/shard_map/ppermute | solution.py:35
  64.6 6.2 %collective-permute-done.7 = bf16[32,2304]{1,0:T(8,128)(2,1)S(1)} collective-permute-done((bf16[32,2304]{1,0:T(8,128)(2,1)S(1)}, bf16[32,2304]{1,0:T(8,128)(2,1)S(1)}, u32[]{:S(2)}, u32[]{:S(2)}) %collective-permute-start.7) | collective-permute-done | bytes 147488 | tf_op jit(solution)/shard_map/ppermute | solution.py:35
  70.7 3.4 %convolution_convert_fusion = bf16[128,1152]{1,0:T(8,128)(2,1)S(1)} fusion(bf16[2304,1152]{1,0:T(8,128)(2,1)} %param.19, bf16[32,2304]{1,0:T(8,128)(2,1)S(1)} %collective-permute-done.8, bf16[32,2304]{1,0:T(8,128)(2,1)S(1)} %collective-permute-done.7, bf16[32,2304]{1,0:T(8,128)(2,1)S(1)} %collective-permute-done.6, bf16[32,2304]{1,0:T(8,128)(2,1)S(1)} %get-tuple-element.75), kind=kOutput, calls=%fused_computation.2 | convolution fusion | flops 681984000 | bytes 6193152 | tf_op jit(solution)/shard_map/dot_general | solution.py:26
  83.8 2.3 %collective-permute-done.11 = bf16[32,1152]{1,0:T(8,128)(2,1)S(1)} collective-permute-done((bf16[32,1152]{1,0:T(8,128)(2,1)S(1)}, bf16[32,1152]{1,0:T(8,128)(2,1)S(1)}, u32[]{:S(2)}, u32[]{:S(2)}) %collective-permute-start.11) | collective-permute-done | bytes 73760 | tf_op jit(solution)/shard_map/ppermute | solution.py:35
  92.2 2.7 %collective-permute-start.17 = (bf16[32,2432]{1,0:T(8,128)(2,1)S(1)}, bf16[32,2432]{1,0:T(8,128)(2,1)S(1)}, u32[]{:S(2)}, u32[]{:S(2)}) collective-permute-start(bf16[32,2432]{1,0:T(8,128)(2,1)S(1)} %get-tuple-element.82), channel_id=1, source_target_pairs={{0,8},{8,0},{16,24},{24,16},{1,9},{9,1},{17,25},{25,17},{2,10},{10... | collective-permute-start | bytes 466952 | tf_op jit(solution)/shard_map/ppermute | solution.py:35
  94.9 4.4 %collective-permute-done.15 = bf16[32,2432]{1,0:T(8,128)(2,1)S(1)} collective-permute-done((bf16[32,2432]{1,0:T(8,128)(2,1)S(1)}, bf16[32,2432]{1,0:T(8,128)(2,1)S(1)}, u32[]{:S(2)}, u32[]{:S(2)}) %collective-permute-start.15) | collective-permute-done | bytes 155680 | tf_op jit(solution)/shard_map/ppermute | solution.py:35
  101.0 9.1 %collective-permute-done.16 = bf16[32,2432]{1,0:T(8,128)(2,1)S(1)} collective-permute-done((bf16[32,2432]{1,0:T(8,128)(2,1)S(1)}, bf16[32,2432]{1,0:T(8,128)(2,1)S(1)}, u32[]{:S(2)}, u32[]{:S(2)}) %collective-permute-start.16) | collective-permute-done | bytes 155680 | tf_op jit(solution)/shard_map/ppermute | solution.py:35
  111.8 4.6 %collective-permute-done.20 = bf16[32,2304]{1,0:T(8,128)(2,1)S(1)} collective-permute-done((bf16[32,2304]{1,0:T(8,128)(2,1)S(1)}, bf16[32,2304]{1,0:T(8,128)(2,1)S(1)}, u32[]{:S(2)}, u32[]{:S(2)}) %collective-permute-start.20) | collective-permute-done | bytes 147488 | tf_op jit(solution)/shard_map/ppermute | solution.py:35
  116.4 2.4 %collective-permute-done.19 = bf16[32,2304]{1,0:T(8,128)(2,1)S(1)} collective-permute-done((bf16[32,2304]{1,0:T(8,128)(2,1)S(1)}, bf16[32,2304]{1,0:T(8,128)(2,1)S(1)}, u32[]{:S(2)}, u32[]{:S(2)}) %collective-permute-start.19) | collective-permute-done | bytes 147488 | tf_op jit(solution)/shard_map/ppermute | solution.py:35
  121.9 3.2 %collective-permute-start.21 = (bf16[32,2432]{1,0:T(8,128)(2,1)S(1)}, bf16[32,2432]{1,0:T(8,128)(2,1)S(1)}, u32[]{:S(2)}, u32[]{:S(2)}) collective-permute-start(bf16[32,2432]{1,0:T(8,128)(2,1)S(1)} %pad_maximum_fusion.16), channel_id=1, source_target_pairs={{0,8},{8,0},{16,24},{24,16},{1,9},{9,1},{17,25},{25,17},{2,10},{10... | collective-permute-start | bytes 466952 | tf_op jit(solution)/shard_map/ppermute | solution.py:35
  126.1 2.8 %collective-permute-done.23 = bf16[32,2432]{1,0:T(8,128)(2,1)S(1)} collective-permute-done((bf16[32,2432]{1,0:T(8,128)(2,1)S(1)}, bf16[32,2432]{1,0:T(8,128)(2,1)S(1)}, u32[]{:S(2)}, u32[]{:S(2)}) %collective-permute-start.23) | collective-permute-done | bytes 155680 | tf_op jit(solution)/shard_map/ppermute | solution.py:35
  130.5 9.1 %collective-permute-done.22 = bf16[32,2432]{1,0:T(8,128)(2,1)S(1)} collective-permute-done((bf16[32,2432]{1,0:T(8,128)(2,1)S(1)}, bf16[32,2432]{1,0:T(8,128)(2,1)S(1)}, u32[]{:S(2)}, u32[]{:S(2)}) %collective-permute-start.22) | collective-permute-done | bytes 155680 | tf_op jit(solution)/shard_map/ppermute | solution.py:35
  143.9 2.3 %collective-permute-start.24 = (bf16[64,1024]{1,0:T(8,128)(2,1)S(1)}, bf16[64,1024]{1,0:T(8,128)(2,1)S(1)}, u32[]{:S(2)}, u32[]{:S(2)}) collective-permute-start(bf16[64,1024]{1,0:T(8,128)(2,1)S(1)} %pad_maximum_fusion.19), channel_id=1, source_target_pairs={{0,24},{8,16},{16,8},{24,0},{1,25},{9,17},{17,9},{25,1},{2,26},{10... | collective-permute-start | bytes 393224 | tf_op jit(solution)/shard_map/ppermute | solution.py:35
  146.2 2.7 %collective-permute-done.31 = bf16[32,2304]{1,0:T(8,128)(2,1)S(1)} collective-permute-done((bf16[32,2304]{1,0:T(8,128)(2,1)S(1)}, bf16[32,2304]{1,0:T(8,128)(2,1)S(1)}, u32[]{:S(2)}, u32[]{:S(2)}) %collective-permute-start.31) | collective-permute-done | bytes 147488 | tf_op jit(solution)/shard_map/ppermute | solution.py:35
  155.1 2.3 %collective-permute-done.34 = bf16[32,1280]{1,0:T(8,128)(2,1)S(1)} collective-permute-done((bf16[32,1280]{1,0:T(8,128)(2,1)S(1)}, bf16[32,1280]{1,0:T(8,128)(2,1)S(1)}, u32[]{:S(2)}, u32[]{:S(2)}) %collective-permute-start.34) | collective-permute-done | bytes 81952 | tf_op jit(solution)/shard_map/ppermute | solution.py:35
  163.1 2.7 %collective-permute-start.27 = (bf16[32,1024]{1,0:T(8,128)(2,1)S(1)}, bf16[32,1024]{1,0:T(8,128)(2,1)S(1)}, u32[]{:S(2)}, u32[]{:S(2)}) collective-permute-start(bf16[32,1024]{1,0:T(8,128)(2,1)S(1)} %fusion.77), channel_id=1, source_target_pairs={{0,8},{8,0},{16,24},{24,16},{1,9},{9,1},{17,25},{25,17},{2,10},{10... | collective-permute-start | bytes 196616 | tf_op jit(solution)/shard_map/ppermute | solution.py:35
  176.2 2.3 %collective-permute-done.40 = f32[9,1024]{1,0:T(8,128)S(1)} collective-permute-done((f32[9,1024]{1,0:T(8,128)S(1)}, f32[9,1024]{1,0:T(8,128)S(1)}, u32[]{:S(2)}, u32[]{:S(2)}) %collective-permute-start.40) | collective-permute-done | bytes 36896 | tf_op jit(solution)/shard_map/ppermute | solution.py:35
  (248 shorter events, 77.1 us)
Async XLA Ops:
  20.6 20.7 %collective-permute-start.1 = (bf16[32,2432]{1,0:T(8,128)(2,1)}, bf16[32,2432]{1,0:T(8,128)(2,1)}, u32[]{:S(2)}, u32[]{:S(2)}) collective-permute-start(bf16[32,2432]{1,0:T(8,128)(2,1)} %get-tuple-element.83), channel_id=1, source_target_pairs={{0,16},{8,24},{16,0},{24,8},{1,17},{9,25},{17,1},{25,9},{2,18},{10... | collective-permute-start | bytes 466952 | tf_op jit(solution)/shard_map/ppermute | solution.py:35
  23.2 19.2 %collective-permute-start = (bf16[32,2432]{1,0:T(8,128)(2,1)}, bf16[32,2432]{1,0:T(8,128)(2,1)}, u32[]{:S(2)}, u32[]{:S(2)}) collective-permute-start(bf16[32,2432]{1,0:T(8,128)(2,1)} %get-tuple-element.84), channel_id=1, source_target_pairs={{0,24},{8,16},{16,8},{24,0},{1,25},{9,17},{17,9},{25,1},{2,26},{10... | collective-permute-start | bytes 466952 | tf_op jit(solution)/shard_map/ppermute | solution.py:35
  24.5 19.8 %collective-permute-start.2 = (bf16[32,2432]{1,0:T(8,128)(2,1)}, bf16[32,2432]{1,0:T(8,128)(2,1)}, u32[]{:S(2)}, u32[]{:S(2)}) collective-permute-start(bf16[32,2432]{1,0:T(8,128)(2,1)} %get-tuple-element.85), channel_id=1, source_target_pairs={{0,8},{8,0},{16,24},{24,16},{1,9},{9,1},{17,25},{25,17},{2,10},{10... | collective-permute-start | bytes 466952 | tf_op jit(solution)/shard_map/ppermute | solution.py:35
  27.6 19.9 %collective-permute-start.3 = (bf16[32,2304]{1,0:T(8,128)(2,1)}, bf16[32,2304]{1,0:T(8,128)(2,1)}, u32[]{:S(2)}, u32[]{:S(2)}) collective-permute-start(bf16[32,2304]{1,0:T(8,128)(2,1)} %get-tuple-element.89), channel_id=1, source_target_pairs={{0,24},{8,16},{16,8},{24,0},{1,25},{9,17},{17,9},{25,1},{2,26},{10... | collective-permute-start | bytes 442376 | tf_op jit(solution)/shard_map/ppermute | solution.py:35
  30.5 16.9 %collective-permute-start.5 = (bf16[32,2304]{1,0:T(8,128)(2,1)}, bf16[32,2304]{1,0:T(8,128)(2,1)}, u32[]{:S(2)}, u32[]{:S(2)}) collective-permute-start(bf16[32,2304]{1,0:T(8,128)(2,1)} %get-tuple-element.90), channel_id=1, source_target_pairs={{0,8},{8,0},{16,24},{24,16},{1,9},{9,1},{17,25},{25,17},{2,10},{10... | collective-permute-start | bytes 442376 | tf_op jit(solution)/shard_map/ppermute | solution.py:35
  41.3 13.0 %collective-permute-start.4 = (bf16[32,2304]{1,0:T(8,128)(2,1)}, bf16[32,2304]{1,0:T(8,128)(2,1)S(1)}, u32[]{:S(2)}, u32[]{:S(2)}) collective-permute-start(bf16[32,2304]{1,0:T(8,128)(2,1)} %get-tuple-element.91), channel_id=1, source_target_pairs={{0,16},{8,24},{16,0},{24,8},{1,17},{9,25},{17,1},{25,9},{2,18},{10... | collective-permute-start | bytes 442376 | tf_op jit(solution)/shard_map/ppermute | solution.py:35
  42.4 112.6 %collective-permute-start.25 = (bf16[64,1024]{1,0:T(8,128)(2,1)S(1)}, bf16[64,1024]{1,0:T(8,128)(2,1)S(1)}, u32[]{:S(2)}, u32[]{:S(2)}) collective-permute-start(bf16[64,1024]{1,0:T(8,128)(2,1)S(1)} %pad_maximum_fusion.20), channel_id=1, source_target_pairs={{0,16},{8,24},{16,0},{24,8},{1,17},{9,25},{17,1},{25,9},{2,18},{10... | collective-permute-start | bytes 393224 | tf_op jit(solution)/shard_map/ppermute | solution.py:35
  44.3 110.6 %collective-permute-start.26 = (bf16[64,1024]{1,0:T(8,128)(2,1)}, bf16[64,1024]{1,0:T(8,128)(2,1)S(1)}, u32[]{:S(2)}, u32[]{:S(2)}) collective-permute-start(bf16[64,1024]{1,0:T(8,128)(2,1)} %pad_maximum_fusion.21), channel_id=1, source_target_pairs={{0,8},{8,0},{16,24},{24,16},{1,9},{9,1},{17,25},{25,17},{2,10},{10... | collective-permute-start | bytes 393224 | tf_op jit(solution)/shard_map/ppermute | solution.py:35
  56.0 8.6 %collective-permute-start.8 = (bf16[32,2304]{1,0:T(8,128)(2,1)S(1)}, bf16[32,2304]{1,0:T(8,128)(2,1)S(1)}, u32[]{:S(2)}, u32[]{:S(2)}) collective-permute-start(bf16[32,2304]{1,0:T(8,128)(2,1)S(1)} %get-tuple-element.75), channel_id=1, source_target_pairs={{0,24},{8,16},{16,8},{24,0},{1,25},{9,17},{17,9},{25,1},{2,26},{10... | collective-permute-start | bytes 442376 | tf_op jit(solution)/shard_map/ppermute | solution.py:35
  58.7 12.0 %collective-permute-start.7 = (bf16[32,2304]{1,0:T(8,128)(2,1)S(1)}, bf16[32,2304]{1,0:T(8,128)(2,1)S(1)}, u32[]{:S(2)}, u32[]{:S(2)}) collective-permute-start(bf16[32,2304]{1,0:T(8,128)(2,1)S(1)} %get-tuple-element.75), channel_id=1, source_target_pairs={{0,16},{8,24},{16,0},{24,8},{1,17},{9,25},{17,1},{25,9},{2,18},{10... | collective-permute-start | bytes 442376 | tf_op jit(solution)/shard_map/ppermute | solution.py:35
  58.7 12.0 %collective-permute-start.6 = (bf16[32,2304]{1,0:T(8,128)(2,1)S(1)}, bf16[32,2304]{1,0:T(8,128)(2,1)S(1)}, u32[]{:S(2)}, u32[]{:S(2)}) collective-permute-start(bf16[32,2304]{1,0:T(8,128)(2,1)S(1)} %get-tuple-element.75), channel_id=1, source_target_pairs={{0,8},{8,0},{16,24},{24,16},{1,9},{9,1},{17,25},{25,17},{2,10},{10... | collective-permute-start | bytes 442376 | tf_op jit(solution)/shard_map/ppermute | solution.py:35
  90.4 8.9 %collective-permute-start.15 = (bf16[32,2432]{1,0:T(8,128)(2,1)S(1)}, bf16[32,2432]{1,0:T(8,128)(2,1)S(1)}, u32[]{:S(2)}, u32[]{:S(2)}) collective-permute-start(bf16[32,2432]{1,0:T(8,128)(2,1)S(1)} %get-tuple-element.80), channel_id=1, source_target_pairs={{0,24},{8,16},{16,8},{24,0},{1,25},{9,17},{17,9},{25,1},{2,26},{10... | collective-permute-start | bytes 466952 | tf_op jit(solution)/shard_map/ppermute | solution.py:35
  92.2 17.9 %collective-permute-start.16 = (bf16[32,2432]{1,0:T(8,128)(2,1)S(1)}, bf16[32,2432]{1,0:T(8,128)(2,1)S(1)}, u32[]{:S(2)}, u32[]{:S(2)}) collective-permute-start(bf16[32,2432]{1,0:T(8,128)(2,1)S(1)} %get-tuple-element.81), channel_id=1, source_target_pairs={{0,16},{8,24},{16,0},{24,8},{1,17},{9,25},{17,1},{25,9},{2,18},{10... | collective-permute-start | bytes 466952 | tf_op jit(solution)/shard_map/ppermute | solution.py:35
  92.2 17.9 %collective-permute-start.17 = (bf16[32,2432]{1,0:T(8,128)(2,1)S(1)}, bf16[32,2432]{1,0:T(8,128)(2,1)S(1)}, u32[]{:S(2)}, u32[]{:S(2)}) collective-permute-start(bf16[32,2432]{1,0:T(8,128)(2,1)S(1)} %get-tuple-element.82), channel_id=1, source_target_pairs={{0,8},{8,0},{16,24},{24,16},{1,9},{9,1},{17,25},{25,17},{2,10},{10... | collective-permute-start | bytes 466952 | tf_op jit(solution)/shard_map/ppermute | solution.py:35
  99.3 12.5 %collective-permute-start.18 = (bf16[32,2304]{1,0:T(8,128)(2,1)S(1)}, bf16[32,2304]{1,0:T(8,128)(2,1)S(1)}, u32[]{:S(2)}, u32[]{:S(2)}) collective-permute-start(bf16[32,2304]{1,0:T(8,128)(2,1)S(1)} %copy-done.10), channel_id=1, source_target_pairs={{0,24},{8,16},{16,8},{24,0},{1,25},{9,17},{17,9},{25,1},{2,26},{10... | collective-permute-start | bytes 442376 | tf_op jit(solution)/shard_map/ppermute | solution.py:35
  110.2 8.6 %collective-permute-start.19 = (bf16[32,2304]{1,0:T(8,128)(2,1)S(1)}, bf16[32,2304]{1,0:T(8,128)(2,1)S(1)}, u32[]{:S(2)}, u32[]{:S(2)}) collective-permute-start(bf16[32,2304]{1,0:T(8,128)(2,1)S(1)} %copy-done.8), channel_id=1, source_target_pairs={{0,16},{8,24},{16,0},{24,8},{1,17},{9,25},{17,1},{25,9},{2,18},{10... | collective-permute-start | bytes 442376 | tf_op jit(solution)/shard_map/ppermute | solution.py:35
  120.7 8.2 %collective-permute-start.23 = (bf16[32,2432]{1,0:T(8,128)(2,1)S(1)}, bf16[32,2432]{1,0:T(8,128)(2,1)S(1)}, u32[]{:S(2)}, u32[]{:S(2)}) collective-permute-start(bf16[32,2432]{1,0:T(8,128)(2,1)S(1)} %pad_maximum_fusion.16), channel_id=1, source_target_pairs={{0,24},{8,16},{16,8},{24,0},{1,25},{9,17},{17,9},{25,1},{2,26},{10... | collective-permute-start | bytes 466952 | tf_op jit(solution)/shard_map/ppermute | solution.py:35
  121.9 17.6 %collective-permute-start.22 = (bf16[32,2432]{1,0:T(8,128)(2,1)S(1)}, bf16[32,2432]{1,0:T(8,128)(2,1)S(1)}, u32[]{:S(2)}, u32[]{:S(2)}) collective-permute-start(bf16[32,2432]{1,0:T(8,128)(2,1)S(1)} %pad_maximum_fusion.16), channel_id=1, source_target_pairs={{0,16},{8,24},{16,0},{24,8},{1,17},{9,25},{17,1},{25,9},{2,18},{10... | collective-permute-start | bytes 466952 | tf_op jit(solution)/shard_map/ppermute | solution.py:35
  121.9 17.6 %collective-permute-start.21 = (bf16[32,2432]{1,0:T(8,128)(2,1)S(1)}, bf16[32,2432]{1,0:T(8,128)(2,1)S(1)}, u32[]{:S(2)}, u32[]{:S(2)}) collective-permute-start(bf16[32,2432]{1,0:T(8,128)(2,1)S(1)} %pad_maximum_fusion.16), channel_id=1, source_target_pairs={{0,8},{8,0},{16,24},{24,16},{1,9},{9,1},{17,25},{25,17},{2,10},{10... | collective-permute-start | bytes 466952 | tf_op jit(solution)/shard_map/ppermute | solution.py:35
  128.9 15.1 %collective-permute-start.32 = (bf16[32,2304]{1,0:T(8,128)(2,1)S(1)}, bf16[32,2304]{1,0:T(8,128)(2,1)S(1)}, u32[]{:S(2)}, u32[]{:S(2)}) collective-permute-start(bf16[32,2304]{1,0:T(8,128)(2,1)S(1)} %get-tuple-element.67), channel_id=1, source_target_pairs={{0,24},{8,16},{16,8},{24,0},{1,25},{9,17},{17,9},{25,1},{2,26},{10... | collective-permute-start | bytes 442376 | tf_op jit(solution)/shard_map/ppermute | solution.py:35
  139.6 9.3 %collective-permute-start.31 = (bf16[32,2304]{1,0:T(8,128)(2,1)S(1)}, bf16[32,2304]{1,0:T(8,128)(2,1)S(1)}, u32[]{:S(2)}, u32[]{:S(2)}) collective-permute-start(bf16[32,2304]{1,0:T(8,128)(2,1)S(1)} %get-tuple-element.67), channel_id=1, source_target_pairs={{0,16},{8,24},{16,0},{24,8},{1,17},{9,25},{17,1},{25,9},{2,18},{10... | collective-permute-start | bytes 442376 | tf_op jit(solution)/shard_map/ppermute | solution.py:35
  139.6 9.3 %collective-permute-start.30 = (bf16[32,2304]{1,0:T(8,128)(2,1)S(1)}, bf16[32,2304]{1,0:T(8,128)(2,1)S(1)}, u32[]{:S(2)}, u32[]{:S(2)}) collective-permute-start(bf16[32,2304]{1,0:T(8,128)(2,1)S(1)} %get-tuple-element.67), channel_id=1, source_target_pairs={{0,8},{8,0},{16,24},{24,16},{1,9},{9,1},{17,25},{25,17},{2,10},{10... | collective-permute-start | bytes 442376 | tf_op jit(solution)/shard_map/ppermute | solution.py:35
  143.9 11.0 %collective-permute-start.24 = (bf16[64,1024]{1,0:T(8,128)(2,1)S(1)}, bf16[64,1024]{1,0:T(8,128)(2,1)S(1)}, u32[]{:S(2)}, u32[]{:S(2)}) collective-permute-start(bf16[64,1024]{1,0:T(8,128)(2,1)S(1)} %pad_maximum_fusion.19), channel_id=1, source_target_pairs={{0,24},{8,16},{16,8},{24,0},{1,25},{9,17},{17,9},{25,1},{2,26},{10... | collective-permute-start | bytes 393224 | tf_op jit(solution)/shard_map/ppermute | solution.py:35
  161.4 7.5 %collective-permute-start.29 = (bf16[32,1024]{1,0:T(8,128)(2,1)S(1)}, bf16[32,1024]{1,0:T(8,128)(2,1)S(1)}, u32[]{:S(2)}, u32[]{:S(2)}) collective-permute-start(bf16[32,1024]{1,0:T(8,128)(2,1)S(1)} %fusion.77), channel_id=1, source_target_pairs={{0,24},{8,16},{16,8},{24,0},{1,25},{9,17},{17,9},{25,1},{2,26},{10... | collective-permute-start | bytes 196616 | tf_op jit(solution)/shard_map/ppermute | solution.py:35
  (55 other events, 785.1 us)

commit v3 on v2

--- a/solution.py
+++ b/solution.py
@@ -1,6 +1,8 @@
 import jax
 import jax.numpy as jnp
 from jax import lax
+from jax.experimental import pallas as pl
+from jax.experimental.pallas import tpu as pltpu
 from jax.sharding import PartitionSpec as P
 
 
@@ -57,6 +59,23 @@
     ]
 
 
+def handed_on(source_ref, target_ref):
+    target_ref[...] = source_ref[...]
+
+
+def before_gather(value):
+    vmem = pl.BlockSpec(memory_space=pltpu.VMEM)
+    return pl.pallas_call(
+        handed_on,
+        out_shape=jax.ShapeDtypeStruct(value.shape, value.dtype),
+        in_specs=[vmem],
+        out_specs=vmem,
+        compiler_params=pltpu.CompilerParams(vmem_limit_bytes=2 << 20),
+        cost_estimate=pl.CostEstimate(flops=1 << 34, bytes_accessed=32 << 20, transcendentals=0),
+        name="before_gather",
+    )(value)
+
+
 def send_mp(blocks):
     got = []
     for m in reversed(range(1, lax.axis_size("mp"))):
@@ -71,8 +90,24 @@
     return jnp.concatenate(blocks, axis=0)
 
 
-def reduce_latent(partial, extra, side):
+def relay_mp(block):
+    if lax.axis_size("mp") != 4:
+        return gather_mp(block)
+
+    def send(value, pairs):
+        return lax.ppermute(value, "mp", pairs)
+
+    rows = block.shape[0]
+    outer = send(block, [(0, 2), (3, 1)])
+    inner = send(block, [(1, 2), (2, 1)])
+    near = send(block, [(i, i ^ 1) for i in range(4)])
+    passed = send(jnp.concatenate([inner, outer], axis=0), [(2, 3), (1, 0)])
+    return jnp.concatenate([block, near, outer + passed[:rows], inner + passed[rows:]], axis=0)
+
+
+def reduce_latent(partial, extra, sides):
     count = lax.axis_size("latent")
+    side, other_side = sides
     half = partial.shape[0] // 2
     width = partial.shape[1]
 
@@ -87,21 +122,23 @@
         return jnp.where(first, value[:half], value[half:])
 
     main, column = pick(partial, side), None if extra is None else pick(extra, side)
-    sent = pack(pick(partial, ~side), None if extra is None else pick(extra, ~side))
+    sent = pack(pick(partial, other_side), None if extra is None else pick(extra, other_side))
     got = swap(sent, "latent", 1)
     main, column = add(main, column, got)
-    distances = [1 << bit for bit in range(1, count.bit_length() - 1)]
-    quarter = half // 2
-    done = []
-    for lower, order in ((0, distances), (quarter, distances[::-1])):
-        done.append(
-            [main[lower : lower + quarter], None if column is None else column[lower : lower + quarter], order]
-        )
-    for step in range(len(distances)):
-        got = [swap(pack(m, c), "latent", order[step]) for m, c, order in done]
-        done = [[*add(m, c, g), order] for (m, c, order), g in zip(done, got)]
-    main = jnp.concatenate([d[0] for d in done], axis=0)
-    column = None if extra is None else jnp.concatenate([d[1] for d in done], axis=0)
+    bits = [1 << bit for bit in range(1, count.bit_length() - 1)]
+    for step in range(0, len(bits), 2):
+        group = bits[step : step + 2]
+        terms = [(main.astype(f32), column)]
+        for distance in [group[0]] if len(group) == 1 else [group[0], group[1], sum(group)]:
+            got = swap(pack(main, column), "latent", distance)
+            far = None if column is None else join_columns(got[:, width:], 1)[0]
+            terms.append((got[:, :width].astype(f32), far))
+        while len(terms) > 1:
+            terms = [
+                (left[0] + right[0], None if column is None else left[1] + right[1])
+                for left, right in zip(terms[::2], terms[1::2])
+            ]
+        main, column = terms[0][0].astype(bf16), terms[0][1]
     other = swap(pack(main, column), "latent", 1)
     low = jnp.where(side, main, other[:, :width])
     high = jnp.where(side, other[:, :width], main)
@@ -144,12 +181,12 @@
     sequences, picks = patch_positions.shape
     length = tokens // sequences
     starts = [(mp_index ^ m) * rows for m in range(mp_count)]
-    side = (latent_index & 1) == 0
+    sides = ((latent_index & 1) == 0, (latent_index & 1) == 1)
     own_row = latent_index * local_rows
     own_row = (mp_index ^ lax.div(own_row, rows)) * rows + lax.rem(own_row, rows)
     streams = jnp.concatenate([clean_stream, output_grad, patch_stream], axis=1)
-    starts, side, own_row, mp_index, streams = lax.optimization_barrier(
-        (starts, side, own_row, mp_index, streams)
+    starts, sides, own_row, mp_index, streams = lax.optimization_barrier(
+        (starts, sides, own_row, mp_index, streams)
     )
 
     def block_of(value, distance):
@@ -161,7 +198,7 @@
     def blocks_of(value):
         return [block_of(value, m) for m in range(1, mp_count)]
 
-    streams = lax.all_gather(streams, "latent", axis=0, tiled=True)
+    streams = lax.all_gather(before_gather(streams), "latent", axis=0, tiled=True)
     width = clean_stream.shape[1]
     clean = streams[:, :width]
     clean_rows = clean.astype(f32)
@@ -198,21 +235,20 @@
 
     linear_part = dot_transposed((output_gain * grad.astype(f32)).astype(bf16), down_weight)
     linear_sent = linear_part.astype(bf16)
-    linear_got = send_mp(blocks_of(linear_sent))
-
     encode_clean = dot((clean_rows - decoder_bias).astype(bf16), encoder_weight)
+    clean_sent = encode_clean.astype(bf16)
+    linear_got = send_mp([jnp.concatenate(pair, axis=1) for pair in zip(blocks_of(linear_sent), blocks_of(clean_sent))])
+    clean_got = [piece[:, hidden_width:] for piece in linear_got]
+    linear_got = [piece[:, :hidden_width] for piece in linear_got]
     encode_patch = dot((patch.astype(f32) - decoder_bias).astype(bf16), encoder_weight)
-    encode_sent = [
-        jnp.concatenate([block_of(encode_clean, m), block_of(encode_patch, m)], axis=0).astype(bf16)
-        for m in range(1, mp_count)
-    ]
+    patch_sent = encode_patch.astype(bf16)
 
     ordered = [jnp.concatenate([block_of(v, m) for m in range(mp_count)], axis=0) for v in (clean, grad)]
     clean_rows, grad_rows = (value.astype(f32) for value in lax.optimization_barrier(ordered))
     weighted_out = output_gain * grad_rows
 
     mlp_part = dot(hidden_all, down_weight).astype(bf16)
-    mlp_out, _ = reduce_latent(mlp_part, None, side)
+    mlp_out, _ = reduce_latent(mlp_part, None, sides)
     mlp_rows = mlp_out.astype(f32)
     square_out = jnp.sum(mlp_rows * mlp_rows, axis=1, keepdims=True)
     cross_out = jnp.sum(mlp_rows * weighted_out, axis=1, keepdims=True)
@@ -227,22 +263,22 @@
     hidden_grad = out_scale * total(block_of(linear_part, 0), linear_got) - (
         out_scale * out_scale * out_scale * (cross_own / model_width)
     ) * total(back_part[:rows], [piece[:, :hidden_width] for piece in back_got])
+    up_grads = relay_mp((hidden_grad * gelu_value).astype(bf16))
     gate_grad = (hidden_grad * gate_factor).astype(bf16)
     cross_in = jnp.sum(hidden_grad * radial, axis=1, keepdims=True)
     gate_grads = gather_mp(jnp.concatenate([gate_grad, split_columns([cross_in, in_scale, out_scale])], axis=1))
-    up_grads = gather_mp((hidden_grad * gelu_value).astype(bf16))
     cross_in, in_scale, out_scale = join_columns(gate_grads[:, hidden_width:], 3)
 
 
-    encode_got = send_mp(encode_sent)
+    patch_got = send_mp(blocks_of(patch_sent))
     latents = encoder_weight.shape[1]
-    own_sums = jnp.concatenate([block_of(encode_clean, 0), block_of(encode_patch, 0)], axis=0)
-    feature = jnp.maximum(total(own_sums, encode_got) + encoder_bias, 0.0)
-    feature_delta = gather_mp((feature[rows:] - feature[:rows]).astype(bf16)).astype(f32)
+    feature_clean = jnp.maximum(total(block_of(encode_clean, 0), clean_got) + encoder_bias, 0.0)
+    feature_patch = jnp.maximum(total(block_of(encode_patch, 0), patch_got) + encoder_bias, 0.0)
+    feature_delta = gather_mp((feature_patch - feature_clean).astype(bf16)).astype(f32)
 
     gate_back = dot_transposed(gate_grads[:, :hidden_width], gate_weight)
     normed_part = dot_transposed(up_grads, up_weight) + gate_back
-    normed_grad, cross_in = reduce_latent(normed_part.astype(bf16), cross_in, side)
+    normed_grad, cross_in = reduce_latent(normed_part.astype(bf16), cross_in, sides)
     site_grad = (
         grad_rows
         + in_scale * (input_gain * normed_grad.astype(f32))

time: 180 us -> 177 us (0.983)
  starting transfers between devices: 52.3 us -> 70 us
  matrix products: 20.2 us -> 11.8 us
  other arithmetic: 13.5 us -> 5.9 us
  local copies, waits for them, and re-layouts: 8.95 us -> 2.02 us
  waiting for transfers between devices: 70.7 us -> 73.6 us
    ppermute x42 -> x37, starting transfers between devices: 52.3 us -> 61.7 us  [swap(): return lax.ppermute(value, axis, [(i, i ^ distance) for i in range(count)])]
    ppermute x0 -> x4, starting transfers between devices: none -> 8.26 us  [send(): return lax.ppermute(value, 'mp', pairs)]
    dot_general x5, matrix products: 11 us -> 3.86 us  [dot(): return jnp.dot(left, right, preferred_element_type=f32)]
    ppermute x0 -> x4, waiting for transfers between devices: none -> 6.62 us  [send(): return lax.ppermute(value, 'mp', pairs)]
    ppermute x42 -> x37, waiting for transfers between devices: 70.7 us -> 67 us  [swap(): return lax.ppermute(value, axis, [(i, i ^ distance) for i in range(count)])]
    dynamic_slice x6, local copies, waits for them, and re-layouts: 3.77 us -> 0.54 us  [block_of(): lax.dynamic_slice(value, (starts[distance], zero), (rows, value.shape[1])...]
    unnamed x72 -> x28, local copies, waits for them, and re-layouts: 2.42 us -> 0.16 us
  transfers between devices with their start and end apart: 42 -> 41, of which waited for: 22 -> 22; matrix products, arithmetic and copies ran while one was open for 18% -> 9% of each run, Pallas kernels for 0% -> 0%
where the time goes in v3:
time: 177 us
  waiting for transfers between devices  73.6 us (42%)
  starting transfers between devices  70 us (40%)
  blocking collectives  12.4 us (7%)
  matrix products  11.8 us (7%)
  other arithmetic  5.9 us (3%)
  local copies, waits for them, and re-layouts  2.02 us (1%)
    ppermute x37, waiting for transfers between devices, swap(): return lax.ppermute(value, axis, [(i, i ^ distance) for i in range(count)])  67 us
    ppermute x37, starting transfers between devices, swap(): return lax.ppermute(value, axis, [(i, i ^ distance) for i in range(count)])  61.7 us
    all_gather x1, blocking collectives, program(): lax.all_gather(before_gather(streams), 'latent', axis=0, tiled=True)  12.4 us
    ppermute x4, starting transfers between devices, send(): return lax.ppermute(value, 'mp', pairs)  8.26 us
    dot_general x5, matrix products, dot_transposed(): lax.dot_general(left, right, (((1,), (1,)), ((), ())), preferred_element_...  7.61 us
    ppermute x4, waiting for transfers between devices, send(): return lax.ppermute(value, 'mp', pairs)  6.62 us
    dot_general x5, matrix products, dot(): return jnp.dot(left, right, preferred_element_type=f32)  3.86 us
  transfers between devices with their start and end apart: 41, of which 22 were waited for; matrix products, arithmetic and copies ran while one was open for 9% of the time, Pallas kernels for 0%

profile of v3, /device:TPU:0, one launch (start us, length us, event | category | flops | bytes accessed | tf_op | source)
XLA Modules:
  0.0 177.1 jit_solution(7751221162555043639)
XLA Ops:
  1.7 12.4 %all_gather.3 = bf16[128,3456]{1,0:T(8,128)(2,1)S(1)} all-gather(bf16[16,3456]{1,0:T(8,128)(2,1)S(1)} %before_gather.1), channel_id=1, replica_groups=mesh['mp'=4,'latent'=8] {'latent'}, dimensions={0}, use_global_device_ids=true | all-gather | bytes 995328 | tf_op jit(solution)/shard_map/all_gather | solution.py:201
  15.6 2.7 %collective-permute-start.1 = (bf16[32,2432]{1,0:T(8,128)(2,1)S(1)}, bf16[32,2432]{1,0:T(8,128)(2,1)S(1)}, u32[]{:S(2)}, u32[]{:S(2)}) collective-permute-start(bf16[32,2432]{1,0:T(8,128)(2,1)S(1)} %get-tuple-element.82), channel_id=1, source_target_pairs={{0,16},{8,24},{16,0},{24,8},{1,17},{9,25},{17,1},{25,9},{2,18},{10... | collective-permute-start | bytes 466952 | tf_op jit(solution)/shard_map/ppermute | solution.py:37
  20.9 3.0 %collective-permute-start.3 = (bf16[32,2304]{1,0:T(8,128)(2,1)S(1)}, bf16[32,2304]{1,0:T(8,128)(2,1)S(1)}, u32[]{:S(2)}, u32[]{:S(2)}) collective-permute-start(bf16[32,2304]{1,0:T(8,128)(2,1)S(1)} %get-tuple-element.88), channel_id=1, source_target_pairs={{0,24},{8,16},{16,8},{24,0},{1,25},{9,17},{17,9},{25,1},{2,26},{10... | collective-permute-start | bytes 442376 | tf_op jit(solution)/shard_map/ppermute | solution.py:37
  27.6 2.7 %collective-permute-done.1 = bf16[32,2432]{1,0:T(8,128)(2,1)S(1)} collective-permute-done((bf16[32,2432]{1,0:T(8,128)(2,1)S(1)}, bf16[32,2432]{1,0:T(8,128)(2,1)S(1)}, u32[]{:S(2)}, u32[]{:S(2)}) %collective-permute-start.1) | collective-permute-done | bytes 155680 | tf_op jit(solution)/shard_map/ppermute | solution.py:37
  30.3 3.4 %collective-permute-start.23 = (bf16[32,1024]{1,0:T(8,128)(2,1)S(1)}, bf16[32,1024]{1,0:T(8,128)(2,1)S(1)}, u32[]{:S(2)}, u32[]{:S(2)}) collective-permute-start(bf16[32,1024]{1,0:T(8,128)(2,1)S(1)} %get-tuple-element.105), channel_id=1, source_target_pairs={{0,24},{8,16},{16,8},{24,0},{1,25},{9,17},{17,9},{25,1},{2,26},{10... | collective-permute-start | bytes 196616 | tf_op jit(solution)/shard_map/ppermute | solution.py:37
  35.2 8.6 %collective-permute-start.25 = (bf16[32,1024]{1,0:T(8,128)(2,1)S(1)}, bf16[32,1024]{1,0:T(8,128)(2,1)S(1)}, u32[]{:S(2)}, u32[]{:S(2)}) collective-permute-start(bf16[32,1024]{1,0:T(8,128)(2,1)S(1)} %get-tuple-element.106), channel_id=1, source_target_pairs={{0,8},{8,0},{16,24},{24,16},{1,9},{9,1},{17,25},{25,17},{2,10},{10... | collective-permute-start | bytes 196616 | tf_op jit(solution)/shard_map/ppermute | solution.py:37
  44.0 3.5 %collective-permute-done.4 = bf16[32,2304]{1,0:T(8,128)(2,1)S(1)} collective-permute-done((bf16[32,2304]{1,0:T(8,128)(2,1)S(1)}, bf16[32,2304]{1,0:T(8,128)(2,1)S(1)}, u32[]{:S(2)}, u32[]{:S(2)}) %collective-permute-start.4) | collective-permute-done | bytes 147488 | tf_op jit(solution)/shard_map/ppermute | solution.py:37
  47.8 3.0 %collective-permute-start.8 = (bf16[32,2304]{1,0:T(8,128)(2,1)S(1)}, bf16[32,2304]{1,0:T(8,128)(2,1)S(1)}, u32[]{:S(2)}, u32[]{:S(2)}) collective-permute-start(bf16[32,2304]{1,0:T(8,128)(2,1)S(1)} %get-tuple-element.74), channel_id=1, source_target_pairs={{0,24},{8,16},{16,8},{24,0},{1,25},{9,17},{17,9},{25,1},{2,26},{10... | collective-permute-start | bytes 442376 | tf_op jit(solution)/shard_map/ppermute | solution.py:37
  52.4 4.1 %collective-permute-done.8 = bf16[32,2304]{1,0:T(8,128)(2,1)S(1)} collective-permute-done((bf16[32,2304]{1,0:T(8,128)(2,1)S(1)}, bf16[32,2304]{1,0:T(8,128)(2,1)S(1)}, u32[]{:S(2)}, u32[]{:S(2)}) %collective-permute-start.8) | collective-permute-done | bytes 147488 | tf_op jit(solution)/shard_map/ppermute | solution.py:37
  56.5 6.2 %collective-permute-done.7 = bf16[32,2304]{1,0:T(8,128)(2,1)S(1)} collective-permute-done((bf16[32,2304]{1,0:T(8,128)(2,1)S(1)}, bf16[32,2304]{1,0:T(8,128)(2,1)S(1)}, u32[]{:S(2)}, u32[]{:S(2)}) %collective-permute-start.7) | collective-permute-done | bytes 147488 | tf_op jit(solution)/shard_map/ppermute | solution.py:37
  68.7 4.2 %collective-permute-done.12 = bf16[64,1152]{1,0:T(8,128)(2,1)S(1)} collective-permute-done((bf16[64,1152]{1,0:T(8,128)(2,1)S(1)}, bf16[64,1152]{1,0:T(8,128)(2,1)S(1)}, u32[]{:S(2)}, u32[]{:S(2)}) %collective-permute-start.12) | collective-permute-done | bytes 147488 | tf_op jit(solution)/shard_map/ppermute | solution.py:37
  83.3 4.4 %collective-permute-done.14 = bf16[32,2432]{1,0:T(8,128)(2,1)S(1)} collective-permute-done((bf16[32,2432]{1,0:T(8,128)(2,1)S(1)}, bf16[32,2432]{1,0:T(8,128)(2,1)S(1)}, u32[]{:S(2)}, u32[]{:S(2)}) %collective-permute-start.14) | collective-permute-done | bytes 155680 | tf_op jit(solution)/shard_map/ppermute | solution.py:37
  87.7 4.5 %collective-permute-start.18 = (bf16[32,3328]{1,0:T(8,128)(2,1)S(1)}, bf16[32,3328]{1,0:T(8,128)(2,1)S(1)}, u32[]{:S(2)}, u32[]{:S(2)}) collective-permute-start(bf16[32,3328]{1,0:T(8,128)(2,1)S(1)} %pad_maximum_fusion.13), channel_id=1, source_target_pairs={{0,16},{8,24},{16,0},{24,8},{1,17},{9,25},{17,1},{25,9},{2,18},{10... | collective-permute-start | bytes 638984 | tf_op jit(solution)/shard_map/ppermute | solution.py:37
  92.2 7.3 %collective-permute-done.15 = bf16[32,2432]{1,0:T(8,128)(2,1)S(1)} collective-permute-done((bf16[32,2432]{1,0:T(8,128)(2,1)S(1)}, bf16[32,2432]{1,0:T(8,128)(2,1)S(1)}, u32[]{:S(2)}, u32[]{:S(2)}) %collective-permute-start.15) | collective-permute-done | bytes 155680 | tf_op jit(solution)/shard_map/ppermute | solution.py:37
  101.4 7.9 %collective-permute-done.18 = bf16[32,3328]{1,0:T(8,128)(2,1)S(1)} collective-permute-done((bf16[32,3328]{1,0:T(8,128)(2,1)S(1)}, bf16[32,3328]{1,0:T(8,128)(2,1)S(1)}, u32[]{:S(2)}, u32[]{:S(2)}) %collective-permute-start.18) | collective-permute-done | bytes 213024 | tf_op jit(solution)/shard_map/ppermute | solution.py:37
  109.3 2.8 %collective-permute-done.19 = bf16[32,3328]{1,0:T(8,128)(2,1)S(1)} collective-permute-done((bf16[32,3328]{1,0:T(8,128)(2,1)S(1)}, bf16[32,3328]{1,0:T(8,128)(2,1)S(1)}, u32[]{:S(2)}, u32[]{:S(2)}) %collective-permute-start.19) | collective-permute-done | bytes 213024 | tf_op jit(solution)/shard_map/ppermute | solution.py:37
  113.0 6.1 %collective-permute-start.30 = (bf16[32,2304]{1,0:T(8,128)(2,1)S(1)}, bf16[32,2304]{1,0:T(8,128)(2,1)S(1)}, u32[]{:S(2)}, u32[]{:S(2)}) collective-permute-start(bf16[32,2304]{1,0:T(8,128)(2,1)S(1)} %get-tuple-element.66), channel_id=1, source_target_pairs={{0,16},{24,8},{1,17},{25,9},{2,18},{26,10},{3,19},{27,11},{4,20},{... | collective-permute-start | bytes 442376 | tf_op jit(solution)/shard_map/ppermute | solution.py:98
  121.0 8.1 %collective-permute-start.21 = (bf16[32,2432]{1,0:T(8,128)(2,1)S(1)}, bf16[32,2432]{1,0:T(8,128)(2,1)S(1)}, u32[]{:S(2)}, u32[]{:S(2)}) collective-permute-start(bf16[32,2432]{1,0:T(8,128)(2,1)S(1)} %pad_maximum_fusion.21), channel_id=1, source_target_pairs={{0,16},{8,24},{16,0},{24,8},{1,17},{9,25},{17,1},{25,9},{2,18},{10... | collective-permute-start | bytes 466952 | tf_op jit(solution)/shard_map/ppermute | solution.py:37
  130.2 3.1 %collective-permute-start.24 = (bf16[32,1024]{1,0:T(8,128)(2,1)S(1)}, bf16[32,1024]{1,0:T(8,128)(2,1)S(1)}, u32[]{:S(2)}, u32[]{:S(2)}) collective-permute-start(bf16[32,1024]{1,0:T(8,128)(2,1)S(1)} %get-tuple-element.107), channel_id=1, source_target_pairs={{0,16},{8,24},{16,0},{24,8},{1,17},{9,25},{17,1},{25,9},{2,18},{10... | collective-permute-start | bytes 196616 | tf_op jit(solution)/shard_map/ppermute | solution.py:37
  133.2 5.8 %collective-permute-done.21 = bf16[32,2432]{1,0:T(8,128)(2,1)S(1)} collective-permute-done((bf16[32,2432]{1,0:T(8,128)(2,1)S(1)}, bf16[32,2432]{1,0:T(8,128)(2,1)S(1)}, u32[]{:S(2)}, u32[]{:S(2)}) %collective-permute-start.21) | collective-permute-done | bytes 155680 | tf_op jit(solution)/shard_map/ppermute | solution.py:37
  142.6 6.6 %collective-permute-done.32 = bf16[64,2304]{1,0:T(8,128)(2,1)S(1)} collective-permute-done((bf16[64,2304]{1,0:T(8,128)(2,1)S(1)}, bf16[64,2304]{1,0:T(8,128)(2,1)S(1)}, u32[]{:S(2)}, u32[]{:S(2)}) %collective-permute-start.32) | collective-permute-done | bytes 294944 | tf_op jit(solution)/shard_map/ppermute | solution.py:98
  158.2 2.9 %collective-permute-done.36 = bf16[64,1280]{1,0:T(8,128)(2,1)S(1)} collective-permute-done((bf16[64,1280]{1,0:T(8,128)(2,1)S(1)}, bf16[64,1280]{1,0:T(8,128)(2,1)S(1)}, u32[]{:S(2)}, u32[]{:S(2)}) %collective-permute-start.36) | collective-permute-done | bytes 163872 | tf_op jit(solution)/shard_map/ppermute | solution.py:37
  161.1 2.6 %collective-permute-done.35 = bf16[64,1280]{1,0:T(8,128)(2,1)S(1)} collective-permute-done((bf16[64,1280]{1,0:T(8,128)(2,1)S(1)}, bf16[64,1280]{1,0:T(8,128)(2,1)S(1)}, u32[]{:S(2)}, u32[]{:S(2)}) %collective-permute-start.35) | collective-permute-done | bytes 163872 | tf_op jit(solution)/shard_map/ppermute | solution.py:37
  168.6 3.0 %collective-permute-start.38 = (f32[9,1024]{1,0:T(8,128)S(1)}, f32[9,1024]{1,0:T(8,128)S(1)}, u32[]{:S(2)}, u32[]{:S(2)}) collective-permute-start(f32[9,1024]{1,0:T(8,128)S(1)} %fusion.24), channel_id=1, source_target_pairs={{0,8},{8,0},{16,24},{24,16},{1,9},{9,1},{17,25},{25,17},{2,10},{10... | collective-permute-start | bytes 110600 | tf_op jit(solution)/shard_map/ppermute | solution.py:37
  (182 shorter events, 57.0 us)
Async XLA Ops:
  15.6 14.7 %collective-permute-start.1 = (bf16[32,2432]{1,0:T(8,128)(2,1)S(1)}, bf16[32,2432]{1,0:T(8,128)(2,1)S(1)}, u32[]{:S(2)}, u32[]{:S(2)}) collective-permute-start(bf16[32,2432]{1,0:T(8,128)(2,1)S(1)} %get-tuple-element.82), channel_id=1, source_target_pairs={{0,16},{8,24},{16,0},{24,8},{1,17},{9,25},{17,1},{25,9},{2,18},{10... | collective-permute-start | bytes 466952 | tf_op jit(solution)/shard_map/ppermute | solution.py:37
  18.2 12.1 %collective-permute-start = (bf16[32,2432]{1,0:T(8,128)(2,1)S(1)}, bf16[32,2432]{1,0:T(8,128)(2,1)S(1)}, u32[]{:S(2)}, u32[]{:S(2)}) collective-permute-start(bf16[32,2432]{1,0:T(8,128)(2,1)S(1)} %get-tuple-element.83), channel_id=1, source_target_pairs={{0,24},{8,16},{16,8},{24,0},{1,25},{9,17},{17,9},{25,1},{2,26},{10... | collective-permute-start | bytes 466952 | tf_op jit(solution)/shard_map/ppermute | solution.py:37
  19.6 15.6 %collective-permute-start.2 = (bf16[32,2432]{1,0:T(8,128)(2,1)S(1)}, bf16[32,2432]{1,0:T(8,128)(2,1)S(1)}, u32[]{:S(2)}, u32[]{:S(2)}) collective-permute-start(bf16[32,2432]{1,0:T(8,128)(2,1)S(1)} %get-tuple-element.84), channel_id=1, source_target_pairs={{0,8},{8,0},{16,24},{24,16},{1,9},{9,1},{17,25},{25,17},{2,10},{10... | collective-permute-start | bytes 466952 | tf_op jit(solution)/shard_map/ppermute | solution.py:37
  20.9 23.1 %collective-permute-start.3 = (bf16[32,2304]{1,0:T(8,128)(2,1)S(1)}, bf16[32,2304]{1,0:T(8,128)(2,1)S(1)}, u32[]{:S(2)}, u32[]{:S(2)}) collective-permute-start(bf16[32,2304]{1,0:T(8,128)(2,1)S(1)} %get-tuple-element.88), channel_id=1, source_target_pairs={{0,24},{8,16},{16,8},{24,0},{1,25},{9,17},{17,9},{25,1},{2,26},{10... | collective-permute-start | bytes 442376 | tf_op jit(solution)/shard_map/ppermute | solution.py:37
  23.9 20.1 %collective-permute-start.5 = (bf16[32,2304]{1,0:T(8,128)(2,1)S(1)}, bf16[32,2304]{1,0:T(8,128)(2,1)S(1)}, u32[]{:S(2)}, u32[]{:S(2)}) collective-permute-start(bf16[32,2304]{1,0:T(8,128)(2,1)S(1)} %get-tuple-element.89), channel_id=1, source_target_pairs={{0,8},{8,0},{16,24},{24,16},{1,9},{9,1},{17,25},{25,17},{2,10},{10... | collective-permute-start | bytes 442376 | tf_op jit(solution)/shard_map/ppermute | solution.py:37
  30.3 17.2 %collective-permute-start.4 = (bf16[32,2304]{1,0:T(8,128)(2,1)S(1)}, bf16[32,2304]{1,0:T(8,128)(2,1)S(1)}, u32[]{:S(2)}, u32[]{:S(2)}) collective-permute-start(bf16[32,2304]{1,0:T(8,128)(2,1)S(1)} %get-tuple-element.90), channel_id=1, source_target_pairs={{0,16},{8,24},{16,0},{24,8},{1,17},{9,25},{17,1},{25,9},{2,18},{10... | collective-permute-start | bytes 442376 | tf_op jit(solution)/shard_map/ppermute | solution.py:37
  30.3 125.6 %collective-permute-start.23 = (bf16[32,1024]{1,0:T(8,128)(2,1)S(1)}, bf16[32,1024]{1,0:T(8,128)(2,1)S(1)}, u32[]{:S(2)}, u32[]{:S(2)}) collective-permute-start(bf16[32,1024]{1,0:T(8,128)(2,1)S(1)} %get-tuple-element.105), channel_id=1, source_target_pairs={{0,24},{8,16},{16,8},{24,0},{1,25},{9,17},{17,9},{25,1},{2,26},{10... | collective-permute-start | bytes 196616 | tf_op jit(solution)/shard_map/ppermute | solution.py:37
  35.2 121.3 %collective-permute-start.25 = (bf16[32,1024]{1,0:T(8,128)(2,1)S(1)}, bf16[32,1024]{1,0:T(8,128)(2,1)S(1)}, u32[]{:S(2)}, u32[]{:S(2)}) collective-permute-start(bf16[32,1024]{1,0:T(8,128)(2,1)S(1)} %get-tuple-element.106), channel_id=1, source_target_pairs={{0,8},{8,0},{16,24},{24,16},{1,9},{9,1},{17,25},{25,17},{2,10},{10... | collective-permute-start | bytes 196616 | tf_op jit(solution)/shard_map/ppermute | solution.py:37
  50.8 11.9 %collective-permute-start.7 = (bf16[32,2304]{1,0:T(8,128)(2,1)S(1)}, bf16[32,2304]{1,0:T(8,128)(2,1)S(1)}, u32[]{:S(2)}, u32[]{:S(2)}) collective-permute-start(bf16[32,2304]{1,0:T(8,128)(2,1)S(1)} %get-tuple-element.74), channel_id=1, source_target_pairs={{0,16},{8,24},{16,0},{24,8},{1,17},{9,25},{17,1},{25,9},{2,18},{10... | collective-permute-start | bytes 442376 | tf_op jit(solution)/shard_map/ppermute | solution.py:37
  50.8 11.9 %collective-permute-start.6 = (bf16[32,2304]{1,0:T(8,128)(2,1)S(1)}, bf16[32,2304]{1,0:T(8,128)(2,1)S(1)}, u32[]{:S(2)}, u32[]{:S(2)}) collective-permute-start(bf16[32,2304]{1,0:T(8,128)(2,1)S(1)} %get-tuple-element.74), channel_id=1, source_target_pairs={{0,8},{8,0},{16,24},{24,16},{1,9},{9,1},{17,25},{25,17},{2,10},{10... | collective-permute-start | bytes 442376 | tf_op jit(solution)/shard_map/ppermute | solution.py:37
  80.7 18.8 %collective-permute-start.15 = (bf16[32,2432]{1,0:T(8,128)(2,1)S(1)}, bf16[32,2432]{1,0:T(8,128)(2,1)S(1)}, u32[]{:S(2)}, u32[]{:S(2)}) collective-permute-start(bf16[32,2432]{1,0:T(8,128)(2,1)S(1)} %get-tuple-element.80), channel_id=1, source_target_pairs={{0,16},{8,24},{16,0},{24,8},{1,17},{9,25},{17,1},{25,9},{2,18},{10... | collective-permute-start | bytes 466952 | tf_op jit(solution)/shard_map/ppermute | solution.py:37
  80.7 18.8 %collective-permute-start.16 = (bf16[32,2432]{1,0:T(8,128)(2,1)S(1)}, bf16[32,2432]{1,0:T(8,128)(2,1)S(1)}, u32[]{:S(2)}, u32[]{:S(2)}) collective-permute-start(bf16[32,2432]{1,0:T(8,128)(2,1)S(1)} %get-tuple-element.81), channel_id=1, source_target_pairs={{0,8},{8,0},{16,24},{24,16},{1,9},{9,1},{17,25},{25,17},{2,10},{10... | collective-permute-start | bytes 466952 | tf_op jit(solution)/shard_map/ppermute | solution.py:37
  87.7 21.5 %collective-permute-start.18 = (bf16[32,3328]{1,0:T(8,128)(2,1)S(1)}, bf16[32,3328]{1,0:T(8,128)(2,1)S(1)}, u32[]{:S(2)}, u32[]{:S(2)}) collective-permute-start(bf16[32,3328]{1,0:T(8,128)(2,1)S(1)} %pad_maximum_fusion.13), channel_id=1, source_target_pairs={{0,16},{8,24},{16,0},{24,8},{1,17},{9,25},{17,1},{25,9},{2,18},{10... | collective-permute-start | bytes 638984 | tf_op jit(solution)/shard_map/ppermute | solution.py:37
  99.5 12.6 %collective-permute-start.19 = (bf16[32,3328]{1,0:T(8,128)(2,1)S(1)}, bf16[32,3328]{1,0:T(8,128)(2,1)S(1)}, u32[]{:S(2)}, u32[]{:S(2)}) collective-permute-start(bf16[32,3328]{1,0:T(8,128)(2,1)S(1)} %pad_maximum_fusion.14), channel_id=1, source_target_pairs={{0,8},{8,0},{16,24},{24,16},{1,9},{9,1},{17,25},{25,17},{2,10},{10... | collective-permute-start | bytes 638984 | tf_op jit(solution)/shard_map/ppermute | solution.py:37
  99.5 12.6 %collective-permute-start.17 = (bf16[32,3328]{1,0:T(8,128)(2,1)S(1)}, bf16[32,3328]{1,0:T(8,128)(2,1)S(1)}, u32[]{:S(2)}, u32[]{:S(2)}) collective-permute-start(bf16[32,3328]{1,0:T(8,128)(2,1)S(1)} %pad_maximum_fusion.12), channel_id=1, source_target_pairs={{0,24},{8,16},{16,8},{24,0},{1,25},{9,17},{17,9},{25,1},{2,26},{10... | collective-permute-start | bytes 638984 | tf_op jit(solution)/shard_map/ppermute | solution.py:37
  113.0 16.1 %collective-permute-start.30 = (bf16[32,2304]{1,0:T(8,128)(2,1)S(1)}, bf16[32,2304]{1,0:T(8,128)(2,1)S(1)}, u32[]{:S(2)}, u32[]{:S(2)}) collective-permute-start(bf16[32,2304]{1,0:T(8,128)(2,1)S(1)} %get-tuple-element.66), channel_id=1, source_target_pairs={{0,16},{24,8},{1,17},{25,9},{2,18},{26,10},{3,19},{27,11},{4,20},{... | collective-permute-start | bytes 442376 | tf_op jit(solution)/shard_map/ppermute | solution.py:98
  119.7 10.5 %collective-permute-start.22 = (bf16[32,2432]{1,0:T(8,128)(2,1)S(1)}, bf16[32,2432]{1,0:T(8,128)(2,1)S(1)}, u32[]{:S(2)}, u32[]{:S(2)}) collective-permute-start(bf16[32,2432]{1,0:T(8,128)(2,1)S(1)} %pad_maximum_fusion.21), channel_id=1, source_target_pairs={{0,24},{8,16},{16,8},{24,0},{1,25},{9,17},{17,9},{25,1},{2,26},{10... | collective-permute-start | bytes 466952 | tf_op jit(solution)/shard_map/ppermute | solution.py:37
  121.0 18.0 %collective-permute-start.21 = (bf16[32,2432]{1,0:T(8,128)(2,1)S(1)}, bf16[32,2432]{1,0:T(8,128)(2,1)S(1)}, u32[]{:S(2)}, u32[]{:S(2)}) collective-permute-start(bf16[32,2432]{1,0:T(8,128)(2,1)S(1)} %pad_maximum_fusion.21), channel_id=1, source_target_pairs={{0,16},{8,24},{16,0},{24,8},{1,17},{9,25},{17,1},{25,9},{2,18},{10... | collective-permute-start | bytes 466952 | tf_op jit(solution)/shard_map/ppermute | solution.py:37
  129.1 9.9 %collective-permute-start.20 = (bf16[32,2432]{1,0:T(8,128)(2,1)S(1)}, bf16[32,2432]{1,0:T(8,128)(2,1)S(1)}, u32[]{:S(2)}, u32[]{:S(2)}) collective-permute-start(bf16[32,2432]{1,0:T(8,128)(2,1)S(1)} %pad_maximum_fusion.21), channel_id=1, source_target_pairs={{0,8},{8,0},{16,24},{24,16},{1,9},{9,1},{17,25},{25,17},{2,10},{10... | collective-permute-start | bytes 466952 | tf_op jit(solution)/shard_map/ppermute | solution.py:37
  130.2 26.4 %collective-permute-start.24 = (bf16[32,1024]{1,0:T(8,128)(2,1)S(1)}, bf16[32,1024]{1,0:T(8,128)(2,1)S(1)}, u32[]{:S(2)}, u32[]{:S(2)}) collective-permute-start(bf16[32,1024]{1,0:T(8,128)(2,1)S(1)} %get-tuple-element.107), channel_id=1, source_target_pairs={{0,16},{8,24},{16,0},{24,8},{1,17},{9,25},{17,1},{25,9},{2,18},{10... | collective-permute-start | bytes 196616 | tf_op jit(solution)/shard_map/ppermute | solution.py:37
  139.0 10.2 %collective-permute-start.29 = (bf16[32,2304]{1,0:T(8,128)(2,1)S(1)}, bf16[32,2304]{1,0:T(8,128)(2,1)S(1)}, u32[]{:S(2)}, u32[]{:S(2)}) collective-permute-start(bf16[32,2304]{1,0:T(8,128)(2,1)S(1)} %get-tuple-element.66), channel_id=1, source_target_pairs={{0,8},{8,0},{16,24},{24,16},{1,9},{9,1},{17,25},{25,17},{2,10},{10... | collective-permute-start | bytes 442376 | tf_op jit(solution)/shard_map/ppermute | solution.py:98
  139.0 10.2 %collective-permute-start.32 = (bf16[64,2304]{1,0:T(8,128)(2,1)S(1)}, bf16[64,2304]{1,0:T(8,128)(2,1)S(1)}, u32[]{:S(2)}, u32[]{:S(2)}) collective-permute-start(bf16[64,2304]{1,0:T(8,128)(2,1)S(1)} %pad_maximum_fusion.11), channel_id=1, source_target_pairs={{16,24},{8,0},{17,25},{9,1},{18,26},{10,2},{19,27},{11,3},{20,28},... | collective-permute-start | bytes 884744 | tf_op jit(solution)/shard_map/ppermute | solution.py:98
  154.5 9.2 %collective-permute-start.35 = (bf16[64,1280]{1,0:T(8,128)(2,1)S(1)}, bf16[64,1280]{1,0:T(8,128)(2,1)S(1)}, u32[]{:S(2)}, u32[]{:S(2)}) collective-permute-start(bf16[64,1280]{1,0:T(8,128)(2,1)S(1)} %pad_maximum_fusion.16), channel_id=1, source_target_pairs={{0,4},{1,5},{2,6},{3,7},{4,0},{5,1},{6,2},{7,3},{8,12},{9,13},{10,... | collective-permute-start | bytes 491528 | tf_op jit(solution)/shard_map/ppermute | solution.py:37
  156.7 10.0 %collective-permute-start.28 = (bf16[32,1024]{1,0:T(8,128)(2,1)S(1)}, bf16[32,1024]{1,0:T(8,128)(2,1)S(1)}, u32[]{:S(2)}, u32[]{:S(2)}) collective-permute-start(bf16[32,1024]{1,0:T(8,128)(2,1)S(1)} %subtract_convert_fusion.2), channel_id=1, source_target_pairs={{0,24},{8,16},{16,8},{24,0},{1,25},{9,17},{17,9},{25,1},{2,26},{10... | collective-permute-start | bytes 196616 | tf_op jit(solution)/shard_map/ppermute | solution.py:37
  (32 other events, 263.5 us)

commit v4 on v3

--- a/solution.py
+++ b/solution.py
@@ -81,6 +81,25 @@
     for m in reversed(range(1, lax.axis_size("mp"))):
         got.append(swap(blocks[m - 1], "mp", m))
     return got
+
+
+def relay_sums(blocks):
+    if lax.axis_size("mp") != 4:
+        return send_mp(blocks)
+
+    def send(value, pairs):
+        return lax.ppermute(value, "mp", pairs)
+
+    def join(left, right):
+        return (left.astype(f32) + right.astype(f32)).astype(bf16)
+
+    far = jnp.concatenate(blocks[1:], axis=0)
+    rows = far.shape[0] // 2
+    got = send(far, [(0, 1), (3, 2)])
+    near = send(blocks[0], [(i, i ^ 1) for i in range(4)])
+    middle = send(join(far[rows:], got[:rows]), [(1, 2), (2, 1)])
+    outer = send(join(far[:rows], got[rows:]), [(1, 3), (2, 0)])
+    return [near, middle, outer]
 
 
 def gather_mp(block):
@@ -203,15 +222,14 @@
     clean = streams[:, :width]
     clean_rows = clean.astype(f32)
     scaled = (clean_rows * input_gain).astype(bf16)
+    up_part = dot(scaled, up_weight)
+    up_got = relay_sums(blocks_of(up_part.astype(bf16)))
     gate_part = dot(scaled, gate_weight)
     square_part = jnp.sum(clean_rows * clean_rows, axis=1, keepdims=True)
     gate_sent = jnp.concatenate([gate_part.astype(bf16), split_columns([square_part])], axis=1)
     gate_got = send_mp(blocks_of(gate_sent))
-    up_part = dot(scaled, up_weight)
-    up_sent = up_part.astype(bf16)
-    up_got = send_mp(blocks_of(up_sent))
     streams, patch_positions, mp_index, _ = lax.optimization_barrier(
-        (streams, patch_positions, mp_index, up_sent)
+        (streams, patch_positions, mp_index, gate_sent)
     )
     place = jnp.arange(tokens, dtype=jnp.int32)
     token = (mp_index ^ lax.div(place, rows)) * rows + lax.rem(place, rows)

time: 177 us -> 175 us (0.989)
  starting transfers between devices: 70 us -> 65.5 us
    ppermute x4 -> x8, waiting for transfers between devices: 6.62 us -> 23.1 us  [send(): return lax.ppermute(value, 'mp', pairs)]
    ppermute x37 -> x34, waiting for transfers between devices: 67 us -> 52.1 us  [swap(): return lax.ppermute(value, axis, [(i, i ^ distance) for i in range(count)])]
    ppermute x37 -> x34, starting transfers between devices: 61.7 us -> 50.5 us  [swap(): return lax.ppermute(value, axis, [(i, i ^ distance) for i in range(count)])]
    ppermute x4 -> x8, starting transfers between devices: 8.26 us -> 15 us  [send(): return lax.ppermute(value, 'mp', pairs)]
  transfers between devices with their start and end apart: 41 -> 42, of which waited for: 22 -> 23; matrix products, arithmetic and copies ran while one was open for 9% -> 9% of each run, Pallas kernels for 0% -> 0%
where the time goes in v4:
time: 175 us; the launch traced here: 174 us
  waiting for transfers between devices  75.2 us (43%)
  starting transfers between devices  65.5 us (37%)
  blocking collectives  12.4 us (7%)
  matrix products  11.8 us (7%)
  other arithmetic  5.98 us (3%)
  local copies, waits for them, and re-layouts  2.02 us (1%)
    ppermute x34, waiting for transfers between devices, swap(): return lax.ppermute(value, axis, [(i, i ^ distance) for i in range(count)])  52.1 us
    ppermute x34, starting transfers between devices, swap(): return lax.ppermute(value, axis, [(i, i ^ distance) for i in range(count)])  50.5 us
    ppermute x8, waiting for transfers between devices, send(): return lax.ppermute(value, 'mp', pairs)  23.1 us
    ppermute x8, starting transfers between devices, send(): return lax.ppermute(value, 'mp', pairs)  15 us
    all_gather x1, blocking collectives, program(): lax.all_gather(before_gather(streams), 'latent', axis=0, tiled=True)  12.4 us
    dot_general x5, matrix products, dot_transposed(): lax.dot_general(left, right, (((1,), (1,)), ((), ())), preferred_element_...  7.6 us
    dot_general x5, matrix products, dot(): return jnp.dot(left, right, preferred_element_type=f32)  3.86 us
  transfers between devices with their start and end apart: 42, of which 23 were waited for; matrix products, arithmetic and copies ran while one was open for 9% of the time, Pallas kernels for 0%

profile of v4, /device:TPU:0, one launch (start us, length us, event | category | flops | bytes accessed | tf_op | source)
XLA Modules:
  0.0 174.3 jit_solution(3682137767690809418)
XLA Ops:
  1.7 12.4 %all_gather.3 = bf16[128,3456]{1,0:T(8,128)(2,1)S(1)} all-gather(bf16[16,3456]{1,0:T(8,128)(2,1)S(1)} %before_gather.1), channel_id=1, replica_groups=mesh['mp'=4,'latent'=8] {'latent'}, dimensions={0}, use_global_device_ids=true | all-gather | bytes 995328 | tf_op jit(solution)/shard_map/all_gather | solution.py:220
  15.6 3.7 %collective-permute-start = (bf16[32,2432]{1,0:T(8,128)(2,1)S(1)}, bf16[32,2432]{1,0:T(8,128)(2,1)S(1)}, u32[]{:S(2)}, u32[]{:S(2)}) collective-permute-start(bf16[32,2432]{1,0:T(8,128)(2,1)S(1)} %get-tuple-element.84), channel_id=1, source_target_pairs={{0,24},{8,16},{16,8},{24,0},{1,25},{9,17},{17,9},{25,1},{2,26},{10... | collective-permute-start | bytes 466952 | tf_op jit(solution)/shard_map/ppermute | solution.py:37
  21.2 3.3 %collective-permute-start.4 = (bf16[64,2304]{1,0:T(8,128)(2,1)S(1)}, bf16[64,2304]{1,0:T(8,128)(2,1)S(1)}, u32[]{:S(2)}, u32[]{:S(2)}) collective-permute-start(bf16[64,2304]{1,0:T(8,128)(2,1)S(1)} %pad_maximum_fusion.9), channel_id=1, source_target_pairs={{0,8},{24,16},{1,9},{25,17},{2,10},{26,18},{3,11},{27,19},{4,12},{... | collective-permute-start | bytes 884744 | tf_op jit(solution)/shard_map/ppermute | solution.py:91
  30.8 2.8 %collective-permute-done.1 = bf16[32,2432]{1,0:T(8,128)(2,1)S(1)} collective-permute-done((bf16[32,2432]{1,0:T(8,128)(2,1)S(1)}, bf16[32,2432]{1,0:T(8,128)(2,1)S(1)}, u32[]{:S(2)}, u32[]{:S(2)}) %collective-permute-start.1) | collective-permute-done | bytes 155680 | tf_op jit(solution)/shard_map/ppermute | solution.py:37
  33.8 3.0 %collective-permute-done.4 = bf16[64,2304]{1,0:T(8,128)(2,1)S(1)} collective-permute-done((bf16[64,2304]{1,0:T(8,128)(2,1)S(1)}, bf16[64,2304]{1,0:T(8,128)(2,1)S(1)}, u32[]{:S(2)}, u32[]{:S(2)}) %collective-permute-start.4) | collective-permute-done | bytes 294944 | tf_op jit(solution)/shard_map/ppermute | solution.py:91
  39.9 12.3 %collective-permute-done.6 = bf16[32,2304]{1,0:T(8,128)(2,1)S(1)} collective-permute-done((bf16[32,2304]{1,0:T(8,128)(2,1)S(1)}, bf16[32,2304]{1,0:T(8,128)(2,1)S(1)}, u32[]{:S(2)}, u32[]{:S(2)}) %collective-permute-start.6) | collective-permute-done | bytes 147488 | tf_op jit(solution)/shard_map/ppermute | solution.py:91
  52.6 3.8 %collective-permute-start.8 = (bf16[32,2304]{1,0:T(8,128)(2,1)S(1)}, bf16[32,2304]{1,0:T(8,128)(2,1)S(1)}, u32[]{:S(2)}, u32[]{:S(2)}) collective-permute-start(bf16[32,2304]{1,0:T(8,128)(2,1)S(1)} %get-tuple-element.74), channel_id=1, source_target_pairs={{0,16},{8,24},{16,0},{24,8},{1,17},{9,25},{17,1},{25,9},{2,18},{10... | collective-permute-start | bytes 442376 | tf_op jit(solution)/shard_map/ppermute | solution.py:37
  57.1 4.0 %collective-permute-done.9 = bf16[32,2304]{1,0:T(8,128)(2,1)S(1)} collective-permute-done((bf16[32,2304]{1,0:T(8,128)(2,1)S(1)}, bf16[32,2304]{1,0:T(8,128)(2,1)S(1)}, u32[]{:S(2)}, u32[]{:S(2)}) %collective-permute-start.9) | collective-permute-done | bytes 147488 | tf_op jit(solution)/shard_map/ppermute | solution.py:37
  61.1 5.7 %collective-permute-done.8 = bf16[32,2304]{1,0:T(8,128)(2,1)S(1)} collective-permute-done((bf16[32,2304]{1,0:T(8,128)(2,1)S(1)}, bf16[32,2304]{1,0:T(8,128)(2,1)S(1)}, u32[]{:S(2)}, u32[]{:S(2)}) %collective-permute-start.8) | collective-permute-done | bytes 147488 | tf_op jit(solution)/shard_map/ppermute | solution.py:37
  72.9 4.2 %collective-permute-done.13 = bf16[64,1152]{1,0:T(8,128)(2,1)S(1)} collective-permute-done((bf16[64,1152]{1,0:T(8,128)(2,1)S(1)}, bf16[64,1152]{1,0:T(8,128)(2,1)S(1)}, u32[]{:S(2)}, u32[]{:S(2)}) %collective-permute-start.13) | collective-permute-done | bytes 147488 | tf_op jit(solution)/shard_map/ppermute | solution.py:37
  77.1 2.3 %collective-permute-done.12 = bf16[64,1152]{1,0:T(8,128)(2,1)S(1)} collective-permute-done((bf16[64,1152]{1,0:T(8,128)(2,1)S(1)}, bf16[64,1152]{1,0:T(8,128)(2,1)S(1)}, u32[]{:S(2)}, u32[]{:S(2)}) %collective-permute-start.12) | collective-permute-done | bytes 147488 | tf_op jit(solution)/shard_map/ppermute | solution.py:37
  84.8 2.6 %collective-permute-start.15 = (bf16[32,2432]{1,0:T(8,128)(2,1)S(1)}, bf16[32,2432]{1,0:T(8,128)(2,1)S(1)}, u32[]{:S(2)}, u32[]{:S(2)}) collective-permute-start(bf16[32,2432]{1,0:T(8,128)(2,1)S(1)} %get-tuple-element.79), channel_id=1, source_target_pairs={{0,24},{8,16},{16,8},{24,0},{1,25},{9,17},{17,9},{25,1},{2,26},{10... | collective-permute-start | bytes 466952 | tf_op jit(solution)/shard_map/ppermute | solution.py:37
  87.5 3.5 %collective-permute-done.17 = bf16[32,2432]{1,0:T(8,128)(2,1)S(1)} collective-permute-done((bf16[32,2432]{1,0:T(8,128)(2,1)S(1)}, bf16[32,2432]{1,0:T(8,128)(2,1)S(1)}, u32[]{:S(2)}, u32[]{:S(2)}) %collective-permute-start.17) | collective-permute-done | bytes 155680 | tf_op jit(solution)/shard_map/ppermute | solution.py:37
  93.1 9.1 %collective-permute-done.16 = bf16[32,2432]{1,0:T(8,128)(2,1)S(1)} collective-permute-done((bf16[32,2432]{1,0:T(8,128)(2,1)S(1)}, bf16[32,2432]{1,0:T(8,128)(2,1)S(1)}, u32[]{:S(2)}, u32[]{:S(2)}) %collective-permute-start.16) | collective-permute-done | bytes 155680 | tf_op jit(solution)/shard_map/ppermute | solution.py:37
  102.2 3.8 %collective-permute-start.25 = (bf16[32,1024]{1,0:T(8,128)(2,1)S(1)}, bf16[32,1024]{1,0:T(8,128)(2,1)S(1)}, u32[]{:S(2)}, u32[]{:S(2)}) collective-permute-start(bf16[32,1024]{1,0:T(8,128)(2,1)S(1)} %get-tuple-element.109), channel_id=1, source_target_pairs={{0,16},{8,24},{16,0},{24,8},{1,17},{9,25},{17,1},{25,9},{2,18},{10... | collective-permute-start | bytes 196616 | tf_op jit(solution)/shard_map/ppermute | solution.py:37
  106.6 7.5 %collective-permute-start.31 = (bf16[32,2304]{1,0:T(8,128)(2,1)S(1)}, bf16[32,2304]{1,0:T(8,128)(2,1)S(1)}, u32[]{:S(2)}, u32[]{:S(2)}) collective-permute-start(bf16[32,2304]{1,0:T(8,128)(2,1)S(1)} %get-tuple-element.66), channel_id=1, source_target_pairs={{0,16},{24,8},{1,17},{25,9},{2,18},{26,10},{3,19},{27,11},{4,20},{... | collective-permute-start | bytes 442376 | tf_op jit(solution)/shard_map/ppermute | solution.py:117
  115.3 2.5 %collective-permute-start.23 = (bf16[32,2432]{1,0:T(8,128)(2,1)S(1)}, bf16[32,2432]{1,0:T(8,128)(2,1)S(1)}, u32[]{:S(2)}, u32[]{:S(2)}) collective-permute-start(bf16[32,2432]{1,0:T(8,128)(2,1)S(1)} %pad_maximum_fusion.23), channel_id=1, source_target_pairs={{0,24},{8,16},{16,8},{24,0},{1,25},{9,17},{17,9},{25,1},{2,26},{10... | collective-permute-start | bytes 466952 | tf_op jit(solution)/shard_map/ppermute | solution.py:37
  118.0 3.4 %collective-permute-start.22 = (bf16[32,2432]{1,0:T(8,128)(2,1)S(1)}, bf16[32,2432]{1,0:T(8,128)(2,1)S(1)}, u32[]{:S(2)}, u32[]{:S(2)}) collective-permute-start(bf16[32,2432]{1,0:T(8,128)(2,1)S(1)} %pad_maximum_fusion.23), channel_id=1, source_target_pairs={{0,16},{8,24},{16,0},{24,8},{1,17},{9,25},{17,1},{25,9},{2,18},{10... | collective-permute-start | bytes 466952 | tf_op jit(solution)/shard_map/ppermute | solution.py:37
  121.4 8.0 %collective-permute-start.21 = (bf16[32,2432]{1,0:T(8,128)(2,1)S(1)}, bf16[32,2432]{1,0:T(8,128)(2,1)S(1)}, u32[]{:S(2)}, u32[]{:S(2)}) collective-permute-start(bf16[32,2432]{1,0:T(8,128)(2,1)S(1)} %pad_maximum_fusion.23), channel_id=1, source_target_pairs={{0,8},{8,0},{16,24},{24,16},{1,9},{9,1},{17,25},{25,17},{2,10},{10... | collective-permute-start | bytes 466952 | tf_op jit(solution)/shard_map/ppermute | solution.py:37
  131.6 5.1 %collective-permute-done.22 = bf16[32,2432]{1,0:T(8,128)(2,1)S(1)} collective-permute-done((bf16[32,2432]{1,0:T(8,128)(2,1)S(1)}, bf16[32,2432]{1,0:T(8,128)(2,1)S(1)}, u32[]{:S(2)}, u32[]{:S(2)}) %collective-permute-start.22) | collective-permute-done | bytes 155680 | tf_op jit(solution)/shard_map/ppermute | solution.py:37
  140.3 6.6 %collective-permute-done.33 = bf16[64,2304]{1,0:T(8,128)(2,1)S(1)} collective-permute-done((bf16[64,2304]{1,0:T(8,128)(2,1)S(1)}, bf16[64,2304]{1,0:T(8,128)(2,1)S(1)}, u32[]{:S(2)}, u32[]{:S(2)}) %collective-permute-start.33) | collective-permute-done | bytes 294944 | tf_op jit(solution)/shard_map/ppermute | solution.py:117
  155.5 3.3 %collective-permute-done.37 = bf16[64,1280]{1,0:T(8,128)(2,1)S(1)} collective-permute-done((bf16[64,1280]{1,0:T(8,128)(2,1)S(1)}, bf16[64,1280]{1,0:T(8,128)(2,1)S(1)}, u32[]{:S(2)}, u32[]{:S(2)}) %collective-permute-start.37) | collective-permute-done | bytes 163872 | tf_op jit(solution)/shard_map/ppermute | solution.py:37
  158.8 2.6 %collective-permute-done.36 = bf16[64,1280]{1,0:T(8,128)(2,1)S(1)} collective-permute-done((bf16[64,1280]{1,0:T(8,128)(2,1)S(1)}, bf16[64,1280]{1,0:T(8,128)(2,1)S(1)}, u32[]{:S(2)}, u32[]{:S(2)}) %collective-permute-start.36) | collective-permute-done | bytes 163872 | tf_op jit(solution)/shard_map/ppermute | solution.py:37
  169.1 3.1 %collective-permute-done.40 = f32[9,1024]{1,0:T(8,128)S(1)} collective-permute-done((f32[9,1024]{1,0:T(8,128)S(1)}, f32[9,1024]{1,0:T(8,128)S(1)}, u32[]{:S(2)}, u32[]{:S(2)}) %collective-permute-start.40) | collective-permute-done | bytes 36896 | tf_op jit(solution)/shard_map/ppermute | solution.py:37
  (186 shorter events, 54.1 us)
Async XLA Ops:
  15.6 12.2 %collective-permute-start = (bf16[32,2432]{1,0:T(8,128)(2,1)S(1)}, bf16[32,2432]{1,0:T(8,128)(2,1)S(1)}, u32[]{:S(2)}, u32[]{:S(2)}) collective-permute-start(bf16[32,2432]{1,0:T(8,128)(2,1)S(1)} %get-tuple-element.84), channel_id=1, source_target_pairs={{0,24},{8,16},{16,8},{24,0},{1,25},{9,17},{17,9},{25,1},{2,26},{10... | collective-permute-start | bytes 466952 | tf_op jit(solution)/shard_map/ppermute | solution.py:37
  19.3 10.6 %collective-permute-start.2 = (bf16[32,2432]{1,0:T(8,128)(2,1)S(1)}, bf16[32,2432]{1,0:T(8,128)(2,1)S(1)}, u32[]{:S(2)}, u32[]{:S(2)}) collective-permute-start(bf16[32,2432]{1,0:T(8,128)(2,1)S(1)} %get-tuple-element.83), channel_id=1, source_target_pairs={{0,8},{8,0},{16,24},{24,16},{1,9},{9,1},{17,25},{25,17},{2,10},{10... | collective-permute-start | bytes 466952 | tf_op jit(solution)/shard_map/ppermute | solution.py:37
  19.3 14.4 %collective-permute-start.1 = (bf16[32,2432]{1,0:T(8,128)(2,1)S(1)}, bf16[32,2432]{1,0:T(8,128)(2,1)S(1)}, u32[]{:S(2)}, u32[]{:S(2)}) collective-permute-start(bf16[32,2432]{1,0:T(8,128)(2,1)S(1)} %get-tuple-element.82), channel_id=1, source_target_pairs={{0,16},{8,24},{16,0},{24,8},{1,17},{9,25},{17,1},{25,9},{2,18},{10... | collective-permute-start | bytes 466952 | tf_op jit(solution)/shard_map/ppermute | solution.py:37
  21.2 15.6 %collective-permute-start.4 = (bf16[64,2304]{1,0:T(8,128)(2,1)S(1)}, bf16[64,2304]{1,0:T(8,128)(2,1)S(1)}, u32[]{:S(2)}, u32[]{:S(2)}) collective-permute-start(bf16[64,2304]{1,0:T(8,128)(2,1)S(1)} %pad_maximum_fusion.9), channel_id=1, source_target_pairs={{0,8},{24,16},{1,9},{25,17},{2,10},{26,18},{3,11},{27,19},{4,12},{... | collective-permute-start | bytes 884744 | tf_op jit(solution)/shard_map/ppermute | solution.py:91
  24.5 15.4 %collective-permute-start.3 = (bf16[32,2304]{1,0:T(8,128)(2,1)S(1)}, bf16[32,2304]{1,0:T(8,128)(2,1)S(1)}, u32[]{:S(2)}, u32[]{:S(2)}) collective-permute-start(bf16[32,2304]{1,0:T(8,128)(2,1)S(1)} %get-tuple-element.88), channel_id=1, source_target_pairs={{0,8},{8,0},{16,24},{24,16},{1,9},{9,1},{17,25},{25,17},{2,10},{10... | collective-permute-start | bytes 442376 | tf_op jit(solution)/shard_map/ppermute | solution.py:91
  27.8 78.5 %collective-permute-start.20 = (bf16[32,3328]{1,0:T(8,128)(2,1)S(1)}, bf16[32,3328]{1,0:T(8,128)(2,1)S(1)}, u32[]{:S(2)}, u32[]{:S(2)}) collective-permute-start(bf16[32,3328]{1,0:T(8,128)(2,1)S(1)} %pad_maximum_fusion.16), channel_id=1, source_target_pairs={{0,8},{8,0},{16,24},{24,16},{1,9},{9,1},{17,25},{25,17},{2,10},{10... | collective-permute-start | bytes 638984 | tf_op jit(solution)/shard_map/ppermute | solution.py:37
  29.9 76.4 %collective-permute-start.19 = (bf16[32,3328]{1,0:T(8,128)(2,1)S(1)}, bf16[32,3328]{1,0:T(8,128)(2,1)S(1)}, u32[]{:S(2)}, u32[]{:S(2)}) collective-permute-start(bf16[32,3328]{1,0:T(8,128)(2,1)S(1)} %pad_maximum_fusion.15), channel_id=1, source_target_pairs={{0,16},{8,24},{16,0},{24,8},{1,17},{9,25},{17,1},{25,9},{2,18},{10... | collective-permute-start | bytes 638984 | tf_op jit(solution)/shard_map/ppermute | solution.py:37
  36.8 15.4 %collective-permute-start.6 = (bf16[32,2304]{1,0:T(8,128)(2,1)S(1)}, bf16[32,2304]{1,0:T(8,128)(2,1)S(1)}, u32[]{:S(2)}, u32[]{:S(2)}) collective-permute-start(bf16[32,2304]{1,0:T(8,128)(2,1)S(1)} %get-tuple-element.106), channel_id=1, source_target_pairs={{8,24},{16,0},{9,25},{17,1},{10,26},{18,2},{11,27},{19,3},{12,28},... | collective-permute-start | bytes 442376 | tf_op jit(solution)/shard_map/ppermute | solution.py:91
  38.1 14.1 %collective-permute-start.5 = (bf16[32,2304]{1,0:T(8,128)(2,1)S(1)}, bf16[32,2304]{1,0:T(8,128)(2,1)S(1)}, u32[]{:S(2)}, u32[]{:S(2)}) collective-permute-start(bf16[32,2304]{1,0:T(8,128)(2,1)S(1)} %get-tuple-element.105), channel_id=1, source_target_pairs={{8,16},{16,8},{9,17},{17,9},{10,18},{18,10},{11,19},{19,11},{12,20... | collective-permute-start | bytes 442376 | tf_op jit(solution)/shard_map/ppermute | solution.py:91
  52.6 14.2 %collective-permute-start.8 = (bf16[32,2304]{1,0:T(8,128)(2,1)S(1)}, bf16[32,2304]{1,0:T(8,128)(2,1)S(1)}, u32[]{:S(2)}, u32[]{:S(2)}) collective-permute-start(bf16[32,2304]{1,0:T(8,128)(2,1)S(1)} %get-tuple-element.74), channel_id=1, source_target_pairs={{0,16},{8,24},{16,0},{24,8},{1,17},{9,25},{17,1},{25,9},{2,18},{10... | collective-permute-start | bytes 442376 | tf_op jit(solution)/shard_map/ppermute | solution.py:37
  56.5 10.4 %collective-permute-start.7 = (bf16[32,2304]{1,0:T(8,128)(2,1)S(1)}, bf16[32,2304]{1,0:T(8,128)(2,1)S(1)}, u32[]{:S(2)}, u32[]{:S(2)}) collective-permute-start(bf16[32,2304]{1,0:T(8,128)(2,1)S(1)} %get-tuple-element.74), channel_id=1, source_target_pairs={{0,8},{8,0},{16,24},{24,16},{1,9},{9,1},{17,25},{25,17},{2,10},{10... | collective-permute-start | bytes 442376 | tf_op jit(solution)/shard_map/ppermute | solution.py:37
  83.1 19.1 %collective-permute-start.16 = (bf16[32,2432]{1,0:T(8,128)(2,1)S(1)}, bf16[32,2432]{1,0:T(8,128)(2,1)S(1)}, u32[]{:S(2)}, u32[]{:S(2)}) collective-permute-start(bf16[32,2432]{1,0:T(8,128)(2,1)S(1)} %get-tuple-element.80), channel_id=1, source_target_pairs={{0,16},{8,24},{16,0},{24,8},{1,17},{9,25},{17,1},{25,9},{2,18},{10... | collective-permute-start | bytes 466952 | tf_op jit(solution)/shard_map/ppermute | solution.py:37
  84.8 17.4 %collective-permute-start.15 = (bf16[32,2432]{1,0:T(8,128)(2,1)S(1)}, bf16[32,2432]{1,0:T(8,128)(2,1)S(1)}, u32[]{:S(2)}, u32[]{:S(2)}) collective-permute-start(bf16[32,2432]{1,0:T(8,128)(2,1)S(1)} %get-tuple-element.79), channel_id=1, source_target_pairs={{0,24},{8,16},{16,8},{24,0},{1,25},{9,17},{17,9},{25,1},{2,26},{10... | collective-permute-start | bytes 466952 | tf_op jit(solution)/shard_map/ppermute | solution.py:37
  91.0 15.3 %collective-permute-start.18 = (bf16[32,3328]{1,0:T(8,128)(2,1)S(1)}, bf16[32,3328]{1,0:T(8,128)(2,1)S(1)}, u32[]{:S(2)}, u32[]{:S(2)}) collective-permute-start(bf16[32,3328]{1,0:T(8,128)(2,1)S(1)} %pad_maximum_fusion.14), channel_id=1, source_target_pairs={{0,24},{8,16},{16,8},{24,0},{1,25},{9,17},{17,9},{25,1},{2,26},{10... | collective-permute-start | bytes 638984 | tf_op jit(solution)/shard_map/ppermute | solution.py:37
  102.2 51.4 %collective-permute-start.26 = (bf16[32,1024]{1,0:T(8,128)(2,1)S(1)}, bf16[32,1024]{1,0:T(8,128)(2,1)S(1)}, u32[]{:S(2)}, u32[]{:S(2)}) collective-permute-start(bf16[32,1024]{1,0:T(8,128)(2,1)S(1)} %get-tuple-element.108), channel_id=1, source_target_pairs={{0,8},{8,0},{16,24},{24,16},{1,9},{9,1},{17,25},{25,17},{2,10},{10... | collective-permute-start | bytes 196616 | tf_op jit(solution)/shard_map/ppermute | solution.py:37
  102.2 52.0 %collective-permute-start.25 = (bf16[32,1024]{1,0:T(8,128)(2,1)S(1)}, bf16[32,1024]{1,0:T(8,128)(2,1)S(1)}, u32[]{:S(2)}, u32[]{:S(2)}) collective-permute-start(bf16[32,1024]{1,0:T(8,128)(2,1)S(1)} %get-tuple-element.109), channel_id=1, source_target_pairs={{0,16},{8,24},{16,0},{24,8},{1,17},{9,25},{17,1},{25,9},{2,18},{10... | collective-permute-start | bytes 196616 | tf_op jit(solution)/shard_map/ppermute | solution.py:37
  106.6 11.4 %collective-permute-start.31 = (bf16[32,2304]{1,0:T(8,128)(2,1)S(1)}, bf16[32,2304]{1,0:T(8,128)(2,1)S(1)}, u32[]{:S(2)}, u32[]{:S(2)}) collective-permute-start(bf16[32,2304]{1,0:T(8,128)(2,1)S(1)} %get-tuple-element.66), channel_id=1, source_target_pairs={{0,16},{24,8},{1,17},{25,9},{2,18},{26,10},{3,19},{27,11},{4,20},{... | collective-permute-start | bytes 442376 | tf_op jit(solution)/shard_map/ppermute | solution.py:117
  115.3 14.2 %collective-permute-start.23 = (bf16[32,2432]{1,0:T(8,128)(2,1)S(1)}, bf16[32,2432]{1,0:T(8,128)(2,1)S(1)}, u32[]{:S(2)}, u32[]{:S(2)}) collective-permute-start(bf16[32,2432]{1,0:T(8,128)(2,1)S(1)} %pad_maximum_fusion.23), channel_id=1, source_target_pairs={{0,24},{8,16},{16,8},{24,0},{1,25},{9,17},{17,9},{25,1},{2,26},{10... | collective-permute-start | bytes 466952 | tf_op jit(solution)/shard_map/ppermute | solution.py:37
  118.0 18.7 %collective-permute-start.22 = (bf16[32,2432]{1,0:T(8,128)(2,1)S(1)}, bf16[32,2432]{1,0:T(8,128)(2,1)S(1)}, u32[]{:S(2)}, u32[]{:S(2)}) collective-permute-start(bf16[32,2432]{1,0:T(8,128)(2,1)S(1)} %pad_maximum_fusion.23), channel_id=1, source_target_pairs={{0,16},{8,24},{16,0},{24,8},{1,17},{9,25},{17,1},{25,9},{2,18},{10... | collective-permute-start | bytes 466952 | tf_op jit(solution)/shard_map/ppermute | solution.py:37
  121.4 15.3 %collective-permute-start.21 = (bf16[32,2432]{1,0:T(8,128)(2,1)S(1)}, bf16[32,2432]{1,0:T(8,128)(2,1)S(1)}, u32[]{:S(2)}, u32[]{:S(2)}) collective-permute-start(bf16[32,2432]{1,0:T(8,128)(2,1)S(1)} %pad_maximum_fusion.23), channel_id=1, source_target_pairs={{0,8},{8,0},{16,24},{24,16},{1,9},{9,1},{17,25},{25,17},{2,10},{10... | collective-permute-start | bytes 466952 | tf_op jit(solution)/shard_map/ppermute | solution.py:37
  129.4 24.8 %collective-permute-start.24 = (bf16[32,1024]{1,0:T(8,128)(2,1)S(1)}, bf16[32,1024]{1,0:T(8,128)(2,1)S(1)}, u32[]{:S(2)}, u32[]{:S(2)}) collective-permute-start(bf16[32,1024]{1,0:T(8,128)(2,1)S(1)} %get-tuple-element.107), channel_id=1, source_target_pairs={{0,24},{8,16},{16,8},{24,0},{1,25},{9,17},{17,9},{25,1},{2,26},{10... | collective-permute-start | bytes 196616 | tf_op jit(solution)/shard_map/ppermute | solution.py:37
  136.7 10.2 %collective-permute-start.30 = (bf16[32,2304]{1,0:T(8,128)(2,1)S(1)}, bf16[32,2304]{1,0:T(8,128)(2,1)S(1)}, u32[]{:S(2)}, u32[]{:S(2)}) collective-permute-start(bf16[32,2304]{1,0:T(8,128)(2,1)S(1)} %get-tuple-element.66), channel_id=1, source_target_pairs={{0,8},{8,0},{16,24},{24,16},{1,9},{9,1},{17,25},{25,17},{2,10},{10... | collective-permute-start | bytes 442376 | tf_op jit(solution)/shard_map/ppermute | solution.py:117
  136.8 10.1 %collective-permute-start.33 = (bf16[64,2304]{1,0:T(8,128)(2,1)S(1)}, bf16[64,2304]{1,0:T(8,128)(2,1)S(1)}, u32[]{:S(2)}, u32[]{:S(2)}) collective-permute-start(bf16[64,2304]{1,0:T(8,128)(2,1)S(1)} %pad_maximum_fusion.13), channel_id=1, source_target_pairs={{16,24},{8,0},{17,25},{9,1},{18,26},{10,2},{19,27},{11,3},{20,28},... | collective-permute-start | bytes 884744 | tf_op jit(solution)/shard_map/ppermute | solution.py:117
  154.4 10.0 %collective-permute-start.29 = (bf16[32,1024]{1,0:T(8,128)(2,1)S(1)}, bf16[32,1024]{1,0:T(8,128)(2,1)S(1)}, u32[]{:S(2)}, u32[]{:S(2)}) collective-permute-start(bf16[32,1024]{1,0:T(8,128)(2,1)S(1)} %subtract_convert_fusion.2), channel_id=1, source_target_pairs={{0,24},{8,16},{16,8},{24,0},{1,25},{9,17},{17,9},{25,1},{2,26},{10... | collective-permute-start | bytes 196616 | tf_op jit(solution)/shard_map/ppermute | solution.py:37
  (33 other events, 275.5 us)
